TPU v7x, 16 devices: a 4x2x1 block of a 4x4x8 slice. The times are simulated.
16 devices in a mesh: rep: 2 (over y, z), pool: 8 (over x, core).
Axes of the slice: x: 4, y: 2, z: 1, core: 2. Of those that a mesh axis runs over, the one named last changes fastest.
The devices are a block of a 4x4x8 slice.
Arguments:
- kv_pool: bfloat16 [3, 1024, 2, 32, 16, 128], P(None, ('rep', 'pool')), parts along dimension 1
- page_idx: int32 [8, 16, 8], P(None, ('rep', 'pool')), parts along dimension 1
- tok_hidden: bfloat16 [16, 64, 2048], P(('rep', 'pool')), parts along dimension 0
- attn_norm: bfloat16 [3, 2048], replicated
- w_query: bfloat16 [3, 2048, 2048], replicated
- w_key: bfloat16 [3, 2048, 2048], replicated
- w_value: bfloat16 [3, 2048, 2048], replicated
- w_out: bfloat16 [3, 2048, 2048], replicated
- mlp_norm: bfloat16 [3, 2048], replicated
- w_gate: bfloat16 [3, 2048, 5504], replicated
- w_up: bfloat16 [3, 2048, 5504], replicated
- w_down: bfloat16 [3, 5504, 2048], replicated
Outputs:
- output: bfloat16 [16, 64, 2048], P(('rep', 'pool')), parts along dimension 0
There are 2 independent parts. A program takes and returns all parts, laid end to end along the dimension named above; an argument that names none is the same for every part.
All inputs are finite; a program needn't handle non-finite values.
Results may differ from a plain program's by a relative error of at most 0.02.
Values are sent between devices in bfloat16 or wider.
A program may use at most 768 MiB of HBM per device.

v0:
```python
import math
import jax
import jax.numpy as jnp
from jax import lax
from jax.sharding import PartitionSpec as P

NORM_EPS = 1e-6
ROPE_BASE = 10000.0


def rms_norm(vals, gain):
    vals_f = vals.astype(jnp.float32)
    inv_rms = lax.rsqrt(jnp.mean(vals_f * vals_f, axis=-1, keepdims=True) + NORM_EPS)
    return (vals_f * inv_rms * gain.astype(jnp.float32)).astype(jnp.bfloat16)


def rope_tables(offset, tokens, head_dim):
    positions = (offset + jnp.arange(tokens)).astype(jnp.float32)
    exponent = jnp.arange(head_dim // 2).astype(jnp.float32) * (-2.0 / head_dim)
    inv_freq = jnp.power(ROPE_BASE, exponent)
    angles = positions[:, None] * inv_freq[None, :]
    return jnp.cos(angles)[:, None, :], jnp.sin(angles)[:, None, :]


def apply_rope(proj, cosine, sine):
    half = proj.shape[-1] // 2
    first = proj[..., :half]
    second = proj[..., half:]
    return jnp.concatenate([first * cosine - second * sine, second * cosine + first * sine], axis=-1)


def attend(query, pages_kv, key_new, val_new):
    tokens = query.shape[-3]
    scale = 1.0 / math.sqrt(query.shape[-1])
    key_pre = pages_kv[..., :, 0, :, :, :]
    val_pre = pages_kv[..., :, 1, :, :, :]
    score_pre = jnp.einsum('...thd,...pshd->...thps', query, key_pre, preferred_element_type=jnp.float32) * scale
    score_new = jnp.einsum('...thd,...uhd->...thu', query, key_new, preferred_element_type=jnp.float32) * scale
    causal = jnp.arange(tokens)[None, :] <= jnp.arange(tokens)[:, None]
    score_new = jnp.where(causal[:, None, :], score_new, -1e30)
    row_max = jnp.maximum(jnp.max(score_pre, axis=(-2, -1)), jnp.max(score_new, axis=-1))
    exp_pre = jnp.exp(score_pre - row_max[..., None, None])
    exp_new = jnp.exp(score_new - row_max[..., None])
    row_sum = jnp.sum(exp_pre, axis=(-2, -1)) + jnp.sum(exp_new, axis=-1)
    prob_pre = (exp_pre / row_sum[..., None, None]).astype(jnp.bfloat16)
    prob_new = (exp_new / row_sum[..., None]).astype(jnp.bfloat16)
    mixed = jnp.einsum('...thps,...pshd->...thd', prob_pre, val_pre, preferred_element_type=jnp.float32)
    mixed = mixed + jnp.einsum('...thu,...uhd->...thd', prob_new, val_new, preferred_element_type=jnp.float32)
    return mixed.astype(jnp.bfloat16)


def decoder_layer(hidden, pages_kv, cosine, sine, layer_weights):
    gain_attn, q_weight, k_weight, v_weight, o_weight, gain_mlp, gate_weight, up_weight, down_weight = layer_weights
    head_shape = hidden.shape[:-1] + pages_kv.shape[-2:]
    normed = rms_norm(hidden, gain_attn)
    query = apply_rope(jnp.dot(normed, q_weight, preferred_element_type=jnp.float32).reshape(head_shape), cosine, sine).astype(jnp.bfloat16)
    key_new = apply_rope(jnp.dot(normed, k_weight, preferred_element_type=jnp.float32).reshape(head_shape), cosine, sine).astype(jnp.bfloat16)
    val_new = jnp.dot(normed, v_weight, preferred_element_type=jnp.float32).astype(jnp.bfloat16).reshape(head_shape)
    mixed = attend(query, pages_kv, key_new, val_new)
    attn_out = mixed.reshape(hidden.shape[:-1] + (q_weight.shape[1],))
    hidden = (hidden.astype(jnp.float32) + jnp.dot(attn_out, o_weight, preferred_element_type=jnp.float32)).astype(jnp.bfloat16)
    normed_mlp = rms_norm(hidden, gain_mlp)
    gate = jnp.dot(normed_mlp, gate_weight, preferred_element_type=jnp.float32)
    upper = jnp.dot(normed_mlp, up_weight, preferred_element_type=jnp.float32)
    inner = (jax.nn.silu(gate) * upper).astype(jnp.bfloat16)
    return (hidden.astype(jnp.float32) + jnp.dot(inner, down_weight, preferred_element_type=jnp.float32)).astype(jnp.bfloat16)


def solution(mesh):
    group = mesh.shape['pool']

    def local_program(kv_local, idx_local, hid_local, attn_norm, w_query, w_key, w_value, w_out, mlp_norm, w_gate, w_up, w_down):
        prefix = group * idx_local.shape[2] * kv_local.shape[3]
        cosine, sine = rope_tables(prefix, hid_local.shape[1], kv_local.shape[-1])
        page_rows = idx_local[:, 0, :].reshape(-1)
        hidden = hid_local[0]
        for layer in range(kv_local.shape[0]):
            outgoing = jnp.take(kv_local[layer], page_rows, axis=0)
            incoming = lax.all_to_all(outgoing, 'pool', 0, 0, tiled=True)
            layer_weights = (attn_norm[layer], w_query[layer], w_key[layer], w_value[layer], w_out[layer], mlp_norm[layer], w_gate[layer], w_up[layer], w_down[layer])
            hidden = decoder_layer(hidden, incoming, cosine, sine, layer_weights)
        return hidden[None]

    data_specs = (P(None, ('rep', 'pool')), P(None, ('rep', 'pool'), None), P(('rep', 'pool')))
    return jax.shard_map(local_program, mesh=mesh, in_specs=data_specs + (P(),) * 9, out_specs=P(('rep', 'pool')), check_vma=False)
```

profile of v0, /device:TPU:113, one launch (start us, length us, event | category | flops | bytes accessed | tf_op | source)
XLA Modules:
  0.0 755.4 jit_solution(3095237936565002457)
XLA Ops:
  0.0 0.5 broadcast.208
  0.5 1.3 reduce.3
  2.0 33.1 %slice_bitcast_fusion = (bf16[64,2,32,16,128]{4,3,2,1,0:T(8,128)(2,1)}, bf16[64,2,32,16,128]{4,3,2,1,0:T(8,128)(2,1)}, bf16[64,2,32,16,128]{4,3,2,1,0:T(8,128)(2,1)}) fusion(bf16[3,64,2,32,16,128]{5,4,3,2,1,0:T(8,128)(2,1)} %param.14), kind=kLoop, calls=%fused_computation.40 | loop fusion | bytes 100663296 | tf_op jit(solution)/shard_map/squeeze | solution.py:78
  35.0 13.5 %gather_fusion.2 = bf16[64,2,32,16,128]{4,3,2,1,0:T(8,128)(2,1)} fusion(bf16[64,2,32,16,128]{4,3,2,1,0:T(8,128)(2,1)} %get-tuple-element.6, s32[1024]{0:T(1024)S(1)} %pad_clamp_fusion), kind=kCustom, calls=%fused_computation.2.clone | custom fusion | bytes 33554688 | tf_op jit(solution)/shard_map/jit(_take)/gather | solution.py:78
  48.5 13.4 %gather_fusion.1 = bf16[64,2,32,16,128]{4,3,2,1,0:T(8,128)(2,1)} fusion(bf16[64,2,32,16,128]{4,3,2,1,0:T(8,128)(2,1)} %get-tuple-element.8, s32[1024]{0:T(1024)S(1)} %pad_clamp_fusion), kind=kCustom, calls=%fused_computation.1.clone | custom fusion | bytes 33554688 | tf_op jit(solution)/shard_map/jit(_take)/gather | solution.py:78
  61.9 13.5 %gather_fusion = bf16[64,2,32,16,128]{4,3,2,1,0:T(8,128)(2,1)} fusion(bf16[64,2,32,16,128]{4,3,2,1,0:T(8,128)(2,1)} %get-tuple-element.7, s32[1024]{0:T(1024)S(1)} %pad_clamp_fusion), kind=kCustom, calls=%fused_computation.clone | custom fusion | bytes 33554688 | tf_op jit(solution)/shard_map/jit(_take)/gather | solution.py:78
  75.3 27.0 %broadcast_select_fusion = (bf16[64,2,32,16,128]{4,3,2,1,0:T(8,128)(2,1)}, bf16[64,2,32,16,128]{4,3,2,1,0:T(8,128)(2,1)}, bf16[64,2,32,16,128]{4,3,2,1,0:T(8,128)(2,1)S(1)}) fusion(bf16[64,2,32,16,128]{4,3,2,1,0:T(8,128)(2,1)} %gather_fusion.2, pred[64]{0:T(512)(128)(4,1)S(1)} %compare_and_fusion, bf16[64,2,32,16,128]{4,3,2,1,0:T(8,128)(2,1)} %gather_fusion.1, ...), kind=kLoop, calls=%fused_computation.45 | loop fusion | flops 25165824 | bytes 100663360 | tf_op jit(solution)/shard_map/jit(_take)/select_n | solution.py:78
  102.3 7.6 %copy.55 = bf16[64,2,32,16,128]{4,2,3,1,0:T(8,128)(2,1)} copy(bf16[64,2,32,16,128]{4,3,2,1,0:T(8,128)(2,1)S(1)} %get-tuple-element.49) | data formatting | bytes 33554432 | tf_op jit(solution)/shard_map/jit(_take)/select_n | solution.py:78
  110.0 7.0 all-to-all-start
  117.0 16.7 %slice_bitcast_fusion.3 = (bf16[2048,2048]{0,1:T(8,128)(2,1)}, bf16[2048,2048]{0,1:T(8,128)(2,1)}, bf16[2048,2048]{0,1:T(8,128)(2,1)}) fusion(bf16[3,2048,2048]{2,1,0:T(8,128)(2,1)} %param.19), kind=kLoop, calls=%fused_computation.77 | loop fusion | bytes 50331648 | tf_op jit(solution)/shard_map/dot_general | solution.py:57
  133.7 12.3 %copy.59 = bf16[2048,2048]{1,0:T(8,128)(2,1)} copy(bf16[2048,2048]{0,1:T(8,128)(2,1)} %get-tuple-element.10) | data formatting | bytes 16777216 | tf_op jit(solution)/shard_map/dot_general | solution.py:57
  146.0 16.7 %slice_bitcast_fusion.4 = (bf16[2048,2048]{0,1:T(8,128)(2,1)}, bf16[2048,2048]{0,1:T(8,128)(2,1)}, bf16[2048,2048]{0,1:T(8,128)(2,1)}) fusion(bf16[3,2048,2048]{2,1,0:T(8,128)(2,1)} %param.18), kind=kLoop, calls=%fused_computation.78 | loop fusion | bytes 50331648 | tf_op jit(solution)/shard_map/dot_general | solution.py:56
  162.8 12.3 %copy.58 = bf16[2048,2048]{1,0:T(8,128)(2,1)} copy(bf16[2048,2048]{0,1:T(8,128)(2,1)} %get-tuple-element.13) | data formatting | bytes 16777216 | tf_op jit(solution)/shard_map/dot_general | solution.py:56
  175.1 12.2 %copy.67 = bf16[2048,2048]{1,0:T(8,128)(2,1)} copy(bf16[2048,2048]{0,1:T(8,128)(2,1)} %get-tuple-element.11) | data formatting | bytes 16777216 | tf_op jit(solution)/shard_map/dot_general | solution.py:57
  187.3 12.3 %copy.66 = bf16[2048,2048]{1,0:T(8,128)(2,1)} copy(bf16[2048,2048]{0,1:T(8,128)(2,1)} %get-tuple-element.14) | data formatting | bytes 16777216 | tf_op jit(solution)/shard_map/dot_general | solution.py:56
  199.6 16.6 %copy.63 = bf16[64,2,32,16,128]{4,2,3,1,0:T(8,128)(2,1)} copy(bf16[64,2,32,16,128]{4,3,2,1,0:T(8,128)(2,1)} %get-tuple-element.48) | data formatting | bytes 33554432 | tf_op jit(solution)/shard_map/jit(_take)/select_n | solution.py:78
  216.2 12.3 %copy.75 = bf16[2048,2048]{1,0:T(8,128)(2,1)} copy(bf16[2048,2048]{0,1:T(8,128)(2,1)} %get-tuple-element.9) | data formatting | bytes 16777216 | tf_op jit(solution)/shard_map/dot_general | solution.py:57
  228.5 12.3 %copy.74 = bf16[2048,2048]{1,0:T(8,128)(2,1)} copy(bf16[2048,2048]{0,1:T(8,128)(2,1)} %get-tuple-element.12) | data formatting | bytes 16777216 | tf_op jit(solution)/shard_map/dot_general | solution.py:56
  240.8 16.7 %copy.71 = bf16[64,2,32,16,128]{4,2,3,1,0:T(8,128)(2,1)} copy(bf16[64,2,32,16,128]{4,3,2,1,0:T(8,128)(2,1)} %get-tuple-element.47) | data formatting | bytes 33554432 | tf_op jit(solution)/shard_map/jit(_take)/select_n | solution.py:78
  257.9 0.6 slice_convert_fusion.1
  258.5 6.0 fusion.201
  264.5 6.1 fusion.203
  270.6 0.5 subtract_convert_fusion.4
  271.1 29.1 %all-to-all-done = bf16[64,2,32,16,128]{4,2,3,1,0:T(8,128)(2,1)} async-done(((bf16[64,2,32,16,128]{4,2,3,1,0:T(8,128)(2,1)}), bf16[64,2,32,16,128]{4,2,3,1,0:T(8,128)(2,1)}, u32[]{:S(2)}, u32[]{:S(2)}) %all-to-all-start) | async-done | bytes 16777248 | tf_op jit(solution)/shard_map/all_to_all | solution.py:79
  300.2 7.3 all-to-all-start.1
  307.5 0.4 fusion.227
  308.0 0.6 slice_convert_fusion
  308.6 5.0 fusion.159
  313.6 10.9 %fusion.226 = (bf16[64,1,32,16,128]{4,2,3,1,0:T(8,128)(2,1)}, bf16[64,1,32,16,128]{4,2,3,1,0:T(8,128)(2,1)S(1)}) fusion(bf16[64,2,32,16,128]{4,2,3,1,0:T(8,128)(2,1)} %all-to-all-done), kind=kLoop, calls=%fused_computation.252 | loop fusion | bytes 33554432 | tf_op jit(solution)/shard_map/slice | solution.py:36
  324.5 7.0 bitcast_reduce_fusion.2
  331.6 9.0 %fusion.30 = f32[64,16]{0,1:T(8,128)S(1)} fusion(f32[16,64,32,64]{3,2,1,0:T(8,128)} %get-tuple-element.51, f32[64,16]{0,1:T(8,128)S(1)} %max.33), kind=kLoop, calls=%fused_computation.48 | loop fusion | flops 6290432 | bytes 8396800 | tf_op jit(solution)/shard_map/reduce_sum | solution.py:44
  340.7 10.2 %fusion.144 = f32[16,128,64]{1,2,0:T(8,128)S(1)} fusion(f32[16,64,32,64]{3,2,1,0:T(8,128)} %get-tuple-element.51, f32[64,16]{0,1:T(8,128)S(1)} %add.206, f32[64,16]{0,1:T(8,128)S(1)} %max.33, bf16[64,1,32,16,128]{4,2,3,1,0:T(8,128)(2,1)} %get-tuple-element.19), kind=kOutput, calls=%fused_computation.126 | convolution fusion | flops 545259520 | bytes 17309696 | tf_op jit(solution)/shard_map/...thps,...pshd->...thd/dot_general | solution.py:47
  351.2 5.1 multiply_reduce_fusion.4
  356.3 10.0 %fusion.16 = f32[64,5504]{1,0:T(8,128)S(1)} fusion(bf16[3,2048,5504]{2,1,0:T(8,128)(2,1)} %param.23, f32[64,2048]{1,0:T(8,128)S(1)} %get-tuple-element.55, f32[2048]{0:T(1024)S(1)} %bitcast.362, f32[64]{0:T(128)S(1)} %add_rsqrt_fusion.4), kind=kOutput, calls=%fused_computation.19 | convolution fusion | flops 1443233792 | bytes 24486144 | tf_op jit(solution)/shard_map/dot_general | solution.py:63
  366.4 10.1 %fusion.72 = bf16[64,5504]{1,0:T(8,128)(2,1)S(1)} fusion(bf16[3,2048,5504]{2,1,0:T(8,128)(2,1)} %param.24, f32[64,5504]{1,0:T(8,128)S(1)} %fusion.16, f32[64,2048]{1,0:T(8,128)S(1)} %get-tuple-element.55, f32[2048]{0:T(1024)S(1)} %bitcast.363, f32[64]{0:T(128)S(1)} %add_rsqrt_fusion.4), kind=kOutput, calls=%fused_computation.92 | convolution fusion | flops 1445347328 | bytes 25190656 | tf_op jit(solution)/shard_map/dot_general | solution.py:64
  376.5 9.7 %multiply_reduce_fusion.3 = (f32[64]{0:T(128)S(1)}, f32[64,2048]{1,0:T(8,128)S(1)}) fusion(f32[64,2048]{1,0:T(8,128)S(1)} %get-tuple-element.55, bf16[64,5504]{1,0:T(8,128)(2,1)S(1)} %fusion.72, bf16[3,5504,2048]{2,1,0:T(8,128)(2,1)} %param.25), kind=kOutput, calls=%fused_computation.163 | convolution fusion | flops 1443495936 | bytes 24297728 | tf_op jit(solution)/shard_map/dot_general | solution.py:66
  386.3 2.7 fusion.197
  389.0 101.9 %all-to-all-done.1 = bf16[64,2,32,16,128]{4,2,3,1,0:T(8,128)(2,1)} async-done(((bf16[64,2,32,16,128]{4,2,3,1,0:T(8,128)(2,1)}), bf16[64,2,32,16,128]{4,2,3,1,0:T(8,128)(2,1)}, u32[]{:S(2)}, u32[]{:S(2)}) %all-to-all-start.1) | async-done | bytes 16777248 | tf_op jit(solution)/shard_map/all_to_all | solution.py:79
  490.9 7.3 all-to-all-start.2
  498.1 10.9 %fusion.225 = (bf16[64,1,32,16,128]{4,2,3,1,0:T(8,128)(2,1)}, bf16[64,1,32,16,128]{4,2,3,1,0:T(8,128)(2,1)S(1)}) fusion(bf16[64,2,32,16,128]{4,2,3,1,0:T(8,128)(2,1)} %all-to-all-done.1), kind=kLoop, calls=%fused_computation.251 | loop fusion | bytes 33554432 | tf_op jit(solution)/shard_map/slice | solution.py:36
  509.0 6.0 fusion.199
  515.5 0.4 fusion.228
  515.9 7.0 bitcast_reduce_fusion.1
  523.1 9.0 %fusion.31 = f32[64,16]{0,1:T(8,128)S(1)} fusion(f32[16,64,32,64]{3,2,1,0:T(8,128)} %get-tuple-element.59, f32[64,16]{0,1:T(8,128)S(1)} %max.34), kind=kLoop, calls=%fused_computation.49 | loop fusion | flops 6290432 | bytes 8396800 | tf_op jit(solution)/shard_map/reduce_sum | solution.py:44
  532.1 5.0 fusion.156
  537.1 10.4 %fusion.145 = f32[16,128,64]{1,2,0:T(8,128)S(1)} fusion(f32[16,64,32,64]{3,2,1,0:T(8,128)} %get-tuple-element.59, f32[64,16]{0,1:T(8,128)S(1)} %add.215, f32[64,16]{0,1:T(8,128)S(1)} %max.34, bf16[64,1,32,16,128]{4,2,3,1,0:T(8,128)(2,1)} %get-tuple-element.17), kind=kOutput, calls=%fused_computation.127 | convolution fusion | flops 545259520 | bytes 17309696 | tf_op jit(solution)/shard_map/...thps,...pshd->...thd/dot_general | solution.py:47
  547.8 5.1 multiply_reduce_fusion.2
  552.9 9.8 %fusion.10 = f32[64,5504]{1,0:T(8,128)S(1)} fusion(bf16[3,2048,5504]{2,1,0:T(8,128)(2,1)} %param.23, f32[64,2048]{1,0:T(8,128)S(1)} %get-tuple-element.63, f32[2048]{0:T(1024)S(1)} %bitcast.360, f32[64]{0:T(128)S(1)} %add_rsqrt_fusion.2), kind=kOutput, calls=%fused_computation.13 | convolution fusion | flops 1443233792 | bytes 24486144 | tf_op jit(solution)/shard_map/dot_general | solution.py:63
  562.7 10.1 %fusion.69 = bf16[64,5504]{1,0:T(8,128)(2,1)S(1)} fusion(bf16[3,2048,5504]{2,1,0:T(8,128)(2,1)} %param.24, f32[64,5504]{1,0:T(8,128)S(1)} %fusion.10, f32[64,2048]{1,0:T(8,128)S(1)} %get-tuple-element.63, f32[2048]{0:T(1024)S(1)} %bitcast.361, f32[64]{0:T(128)S(1)} %add_rsqrt_fusion.2), kind=kOutput, calls=%fused_computation.91 | convolution fusion | flops 1445347328 | bytes 25190656 | tf_op jit(solution)/shard_map/dot_general | solution.py:64
  572.8 9.7 %multiply_reduce_fusion.1 = (f32[64]{0:T(128)S(1)}, f32[64,2048]{1,0:T(8,128)S(1)}) fusion(f32[64,2048]{1,0:T(8,128)S(1)} %get-tuple-element.63, bf16[64,5504]{1,0:T(8,128)(2,1)S(1)} %fusion.69, bf16[3,5504,2048]{2,1,0:T(8,128)(2,1)} %param.25), kind=kOutput, calls=%fused_computation.153 | convolution fusion | flops 1443495936 | bytes 24297728 | tf_op jit(solution)/shard_map/dot_general | solution.py:66
  582.7 2.7 fusion.193
  585.3 6.0 fusion.195
  591.4 0.5 subtract_convert_fusion
  591.8 5.0 fusion.153
  596.8 84.7 %all-to-all-done.2 = bf16[64,2,32,16,128]{4,2,3,1,0:T(8,128)(2,1)} async-done(((bf16[64,2,32,16,128]{4,2,3,1,0:T(8,128)(2,1)}), bf16[64,2,32,16,128]{4,2,3,1,0:T(8,128)(2,1)}, u32[]{:S(2)}, u32[]{:S(2)}) %all-to-all-start.2) | async-done | bytes 16777248 | tf_op jit(solution)/shard_map/all_to_all | solution.py:79
  681.5 11.1 %fusion.224 = (bf16[64,1,32,16,128]{4,2,3,1,0:T(8,128)(2,1)}, bf16[64,1,32,16,128]{4,2,3,1,0:T(8,128)(2,1)S(1)}) fusion(bf16[64,2,32,16,128]{4,2,3,1,0:T(8,128)(2,1)} %all-to-all-done.2), kind=kLoop, calls=%fused_computation.250 | loop fusion | bytes 33554432 | tf_op jit(solution)/shard_map/slice | solution.py:36
  692.6 7.0 bitcast_reduce_fusion
  699.6 0.4 fusion.229
  700.1 9.1 %fusion.32 = f32[64,16]{0,1:T(8,128)S(1)} fusion(f32[16,64,32,64]{3,2,1,0:T(8,128)} %get-tuple-element.67, f32[64,16]{0,1:T(8,128)S(1)} %max.35), kind=kLoop, calls=%fused_computation.50 | loop fusion | flops 6290432 | bytes 8396800 | tf_op jit(solution)/shard_map/reduce_sum | solution.py:44
  709.3 10.2 %fusion.146 = f32[16,128,64]{1,2,0:T(8,128)S(1)} fusion(f32[16,64,32,64]{3,2,1,0:T(8,128)} %get-tuple-element.67, f32[64,16]{0,1:T(8,128)S(1)} %add.224, f32[64,16]{0,1:T(8,128)S(1)} %max.35, bf16[64,1,32,16,128]{4,2,3,1,0:T(8,128)(2,1)} %get-tuple-element.15), kind=kOutput, calls=%fused_computation.128 | convolution fusion | flops 545259520 | bytes 17309696 | tf_op jit(solution)/shard_map/...thps,...pshd->...thd/dot_general | solution.py:47
  719.8 5.1 multiply_reduce_fusion
  724.9 9.6 %fusion.4 = f32[64,5504]{1,0:T(8,128)S(1)} fusion(bf16[3,2048,5504]{2,1,0:T(8,128)(2,1)} %param.23, f32[64,2048]{1,0:T(8,128)S(1)} %get-tuple-element.71, f32[2048]{0:T(1024)S(1)} %bitcast.358, f32[64]{0:T(128)S(1)} %add_rsqrt_fusion), kind=kOutput, calls=%fused_computation.7 | convolution fusion | flops 1443233792 | bytes 24486144 | tf_op jit(solution)/shard_map/dot_general | solution.py:63
  734.6 10.2 %fusion.66 = bf16[64,5504]{1,0:T(8,128)(2,1)S(1)} fusion(bf16[3,2048,5504]{2,1,0:T(8,128)(2,1)} %param.24, f32[64,5504]{1,0:T(8,128)S(1)} %fusion.4, f32[64,2048]{1,0:T(8,128)S(1)} %get-tuple-element.71, f32[2048]{0:T(1024)S(1)} %bitcast.359, f32[64]{0:T(128)S(1)} %add_rsqrt_fusion), kind=kOutput, calls=%fused_computation.90 | convolution fusion | flops 1445347328 | bytes 25190656 | tf_op jit(solution)/shard_map/dot_general | solution.py:64
  744.8 10.3 %fusion.135 = bf16[1,64,2048]{2,1,0:T(8,128)(2,1)} fusion(f32[64,2048]{1,0:T(8,128)S(1)} %get-tuple-element.71, bf16[64,5504]{1,0:T(8,128)(2,1)S(1)} %fusion.66, bf16[3,5504,2048]{2,1,0:T(8,128)(2,1)} %param.25), kind=kOutput, calls=%fused_computation.113 | convolution fusion | flops 1443102720 | bytes 24035328 | tf_op jit(solution)/shard_map/dot_general | solution.py:66
  (52 shorter events, 2.4 us)
Async XLA Ops:
  110.0 190.2 %all-to-all-start = ((bf16[64,2,32,16,128]{4,2,3,1,0:T(8,128)(2,1)}), bf16[64,2,32,16,128]{4,2,3,1,0:T(8,128)(2,1)}, u32[]{:S(2)}, u32[]{:S(2)}) async-start(bf16[64,2,32,16,128]{4,2,3,1,0:T(8,128)(2,1)} %copy.55), calls=%async_computation | async-start | bytes 33554432 | tf_op jit(solution)/shard_map/all_to_all | solution.py:79
  240.8 16.7 %copy-start = (bf16[1,64,2048]{2,1,0:T(8,128)(2,1)S(1)}, bf16[1,64,2048]{2,1,0:T(8,128)(2,1)}, u32[]{:S(2)}) copy-start(bf16[1,64,2048]{2,1,0:T(8,128)(2,1)} %param.16) | copy-start | bytes 786436
  240.8 17.1 %copy-start.1 = (bf16[3,2048]{1,0:T(4,128)(2,1)S(1)}, bf16[3,2048]{1,0:T(4,128)(2,1)}, u32[]{:S(2)}) copy-start(bf16[3,2048]{1,0:T(4,128)(2,1)} %param.17) | copy-start | bytes 36868
  271.1 36.9 %copy-start.2 = (bf16[3,2048]{1,0:T(4,128)(2,1)S(1)}, bf16[3,2048]{1,0:T(4,128)(2,1)}, u32[]{:S(2)}) copy-start(bf16[3,2048]{1,0:T(4,128)(2,1)} %param.22) | copy-start | bytes 36868
  300.2 190.7 %all-to-all-start.1 = ((bf16[64,2,32,16,128]{4,2,3,1,0:T(8,128)(2,1)}), bf16[64,2,32,16,128]{4,2,3,1,0:T(8,128)(2,1)}, u32[]{:S(2)}, u32[]{:S(2)}) async-start(bf16[64,2,32,16,128]{4,2,3,1,0:T(8,128)(2,1)} %copy.63), calls=%async_computation.1 | async-start | bytes 33554432 | tf_op jit(solution)/shard_map/all_to_all | solution.py:79
  356.3 30.0 %slice-start.2 = ((s8[8388608]{0:T(1024)(128)(4,1)}), s8[4194304]{0:T(1024)(128)(4,1)S(1)}, s32[]{:S(2)}) async-start(s8[8388608]{0:T(1024)(128)(4,1)} %bitcast.348), calls=%async_computation.5 | async-start | bytes 8388608
  366.3 20.0 %slice-start.3 = ((s8[8388608]{0:T(1024)(128)(4,1)}), s8[4194304]{0:T(1024)(128)(4,1)S(1)}, s32[]{:S(2)}) async-start(s8[8388608]{0:T(1024)(128)(4,1)} %bitcast.348), calls=%async_computation.6 | async-start | bytes 8388608
  490.9 190.6 %all-to-all-start.2 = ((bf16[64,2,32,16,128]{4,2,3,1,0:T(8,128)(2,1)}), bf16[64,2,32,16,128]{4,2,3,1,0:T(8,128)(2,1)}, u32[]{:S(2)}, u32[]{:S(2)}) async-start(bf16[64,2,32,16,128]{4,2,3,1,0:T(8,128)(2,1)} %copy.71), calls=%async_computation.2 | async-start | bytes 33554432 | tf_op jit(solution)/shard_map/all_to_all | solution.py:79
  537.1 15.8 %copy-start.5 = (f32[1,2048]{1,0:T(1,128)S(1)}, f32[1,2048]{1,0:T(1,128)}, u32[]{:S(2)}) copy-start(f32[1,2048]{1,0:T(1,128)} %get-tuple-element.41) | copy-start | bytes 24580
  552.9 29.8 %slice-start = ((s8[8388608]{0:T(1024)(128)(4,1)}), s8[4194304]{0:T(1024)(128)(4,1)S(1)}, s32[]{:S(2)}) async-start(s8[8388608]{0:T(1024)(128)(4,1)} %bitcast.343), calls=%async_computation.3 | async-start | bytes 8388608
  562.7 20.0 %slice-start.1 = ((s8[8388608]{0:T(1024)(128)(4,1)}), s8[4194304]{0:T(1024)(128)(4,1)S(1)}, s32[]{:S(2)}) async-start(s8[8388608]{0:T(1024)(128)(4,1)} %bitcast.343), calls=%async_computation.4 | async-start | bytes 8388608
  572.8 9.7 %copy-start.3 = (f32[1,2048]{1,0:T(1,128)S(1)}, f32[1,2048]{1,0:T(1,128)}, u32[]{:S(2)}) copy-start(f32[1,2048]{1,0:T(1,128)} %get-tuple-element.42) | copy-start | bytes 24580
  709.3 15.7 %copy-start.4 = (f32[1,2048]{1,0:T(1,128)S(1)}, f32[1,2048]{1,0:T(1,128)}, u32[]{:S(2)}) copy-start(f32[1,2048]{1,0:T(1,128)} %get-tuple-element.39) | copy-start | bytes 24580
where the time goes:
time: 763 us; the launch traced here: 755 us
  local copies, waits for them, and re-layouts  255 us (33%)
  waiting for transfers between devices  216 us (28%)
  matrix products  203 us (27%)
  other arithmetic  59.1 us (8%)
  starting transfers between devices  21.6 us (3%)
    all_to_all x3, waiting for transfers between devices, local_program(): incoming = lax.all_to_all(outgoing, 'pool', 0, 0, tiled=True)  216 us
    dot_general x4, local copies, waits for them, and re-layouts, decoder_layer(): jnp.dot(normed, q_weight, preferred_element_type=jnp.float32)  53.7 us
    dot_general x4, local copies, waits for them, and re-layouts, decoder_layer(): jnp.dot(normed, k_weight, preferred_element_type=jnp.float32)  53.5 us
    select_n x3, local copies, waits for them, and re-layouts, local_program(): outgoing = jnp.take(kv_local[layer], page_rows, axis=0)  40.9 us
    gather x3, local copies, waits for them, and re-layouts, local_program(): outgoing = jnp.take(kv_local[layer], page_rows, axis=0)  40.3 us
    squeeze x1, local copies, waits for them, and re-layouts, local_program(): outgoing = jnp.take(kv_local[layer], page_rows, axis=0)  33.1 us
    slice x3, local copies, waits for them, and re-layouts, attend(): val_pre = pages_kv[..., :, 1, :, :, :]  32.9 us
    dot_general x3, matrix products, attend(): jnp.einsum('...thps,...pshd->...thd', prob_pre, val_pre, preferred_elemen...  30.8 us
  transfers between devices with their start and end apart: 3, of which 3 were waited for; matrix products, arithmetic and copies ran while one was open for 44% of the time, Pallas kernels for 0%

commit v1 on v0

v1 whole, which is shorter than its diff:
```python
import functools
import math
import numpy as np
import jax
import jax.numpy as jnp
from jax import lax
from jax.experimental import pallas as pl
from jax.experimental.pallas import tpu as pltpu
from jax.sharding import PartitionSpec as P

NORM_EPS = 1e-6
ROPE_BASE = 10000.0
LOG2E = 1.4426950408889634
NEG = -1e30
MESH = pl.DeviceIdType.MESH
BF = jnp.bfloat16
F32 = jnp.float32

CORES = 2
CHIPS = 4
COL = 256
PAIRS = 6
STAGE = 8
PITCH = 36
OUT_COL = 512


def rope_tables(offset, tokens, head_dim):
    positions = (offset + np.arange(tokens)).astype(np.float32)
    exponent = np.arange(head_dim // 2).astype(np.float32) * np.float32(-2.0 / head_dim)
    inv_freq = np.power(np.float32(ROPE_BASE), exponent).astype(np.float32)
    angles = (positions[:, None] * inv_freq[None, :]).astype(np.float32)
    cosine, sine = np.cos(angles), np.sin(angles)
    return np.concatenate([cosine, cosine], 1), np.concatenate([-sine, sine], 1)


def kernel(cfg, idx, hid, cos, sin, gain_a, gain_m, kv, wq, wk, wv, wo, wg, wu, wd, out,
           x, h, att, inner, q, k_new, v_new, pages, stage, unpack,
           p_loc, p_send, p_recv, s_loc, s_send, s_recv, n_o, n_s,
           f_o, f_s, fin_o, fin_s, px_send, px_recv, ring, wo_buf, wd_buf,
           ring_sem, wo_sem, wd_sem, stage_sem,
           x_sem, qp_sem, qr_sem, ql_sem, po_sem, ro_sem, lo_sem, px_sem):
    layers, tokens, dim, heads, hd, ff, n_pages, slots = cfg
    group = CORES * CHIPS
    half = heads // CORES
    part = half // 2
    rows = CORES * tokens
    width = half * hd
    ff_cols = wd_buf.shape[1]
    ff_chunks = ff_cols // COL
    overlap = CORES * ff_cols - ff
    me = lax.axis_index("pool")
    chip = lax.div(me, CORES)
    core = lax.rem(me, CORES)
    partner = me + 1 - 2 * core
    right = lax.rem(me + CORES, group)
    left = lax.rem(me + group - CORES, group)
    c_right = lax.rem(chip + 1, CHIPS)
    c_left = lax.rem(chip + CHIPS - 1, CHIPS)
    c_far = lax.rem(chip + 2, CHIPS)
    other = 1 - core
    OWN, RIGHT, LEFT, FAR = 0, 1, 2, 3
    chip_of = {OWN: chip, RIGHT: c_right, LEFT: c_left, FAR: c_far}
    score_scale = LOG2E / math.sqrt(hd)

    def remote(src, dst, sem, dev):
        return pltpu.make_async_remote_copy(src_ref=src, dst_ref=dst, send_sem=sem.at[0], recv_sem=sem.at[1],
                                            device_id={"pool": dev}, device_id_type=MESH)

    def qkv_copy(l, t, w, sub):
        base = lax.rem(t, 2) * 2 * COL + sub * COL
        col = pl.multiple_of(core * width + base, COL)
        slot = 2 * t + sub
        return pltpu.make_async_copy(w.at[l, :, pl.ds(col, COL)], ring.at[slot], ring_sem.at[slot])

    def start_qkv(l, t):
        for n, w in enumerate((wq, wk, wv)):
            @pl.when(lax.div(t, 2) == n)
            def _(w=w):
                for sub in range(2):
                    qkv_copy(l, t, w, sub).start()

    def gu_copy(l, j, sub):
        col = pl.multiple_of(core * (ff - ff_cols) + j * COL, 128)
        slot = 2 * lax.rem(j, PAIRS) + sub
        return pltpu.make_async_copy((wg, wu)[sub].at[l, :, pl.ds(col, COL)], ring.at[slot], ring_sem.at[slot])

    def wo_copy(l, n):
        return pltpu.make_async_copy(wo.at[l, pl.ds(pl.multiple_of(core * width, width), width), pl.ds(pl.multiple_of(n * OUT_COL, OUT_COL), OUT_COL)],
                                     wo_buf.at[n], wo_sem.at[n])

    def wd_copy(l, n):
        row = pl.multiple_of(core * (ff - ff_cols), 128)
        return pltpu.make_async_copy(wd.at[l, pl.ds(row, ff_cols), pl.ds(pl.multiple_of(n * COL, COL), COL)],
                                     wd_buf.at[n], wd_sem.at[n])

    page_len = kv.shape[3]

    def page_copy(l, p):
        s = lax.rem(p, STAGE)
        return pltpu.make_async_copy(kv.at[l, p], stage.at[s], stage_sem.at[s])

    def turn_pages(l, lo, hi):
        def body(p, carry):
            page_copy(l, p).wait()
            s = lax.rem(p, STAGE)
            for b in range(2):
                for r in range(page_len):
                    unpack[b, pl.ds(r, heads, stride=PITCH), :] = stage[s, b, r].astype(F32)
            for b in range(2):
                for i in range(heads):
                    pages[p, b, i] = unpack[b, pl.ds(i * PITCH, page_len), :].astype(BF)
            nxt = p + STAGE

            @pl.when(nxt < n_pages)
            def _():
                page_copy(l, nxt).start()

            @pl.when((nxt >= n_pages) & (l + 1 < layers))
            def _():
                page_copy(l + 1, nxt - n_pages).start()
            return carry
        lax.fori_loop(lo, hi, body, 0)

    def q_right(n):
        src = (q.at[chip, core, 0], q.at[chip, core, 1], q.at[c_left, core, 0])[n]
        return remote(src, src, qr_sem.at[n], right)

    def q_left(n):
        src = (q.at[chip, core, 1], q.at[chip, core, 0], q.at[c_right, core, 1])[n]
        return remote(src, src, ql_sem.at[n], left)

    def q_part(n):
        src = (q.at[chip, core, 0], q.at[chip, core, 1], q.at[c_left, core, 0], q.at[c_left, core, 1],
               q.at[c_right, core, 0], q.at[c_right, core, 1], q.at[c_far, core, 0], q.at[c_far, core, 1])[n]
        return remote(src, src, qp_sem.at[n], partner)

    def o_part(d):
        return (remote(p_send.at[d], p_recv.at[d], po_sem.at[d, 0], partner),
                remote(s_send.at[d], s_recv.at[d], po_sem.at[d, 1], partner))

    def o_right(n):
        d, j, dst_o, dst_s = ((RIGHT, 1, fin_o.at[0, 1], fin_s.at[0, 1]), (FAR, 0, f_o.at[0], f_s.at[0]),
                              (RIGHT, 0, fin_o.at[0, 0], fin_s.at[0, 0]))[n]
        return (remote(p_loc.at[d, j], dst_o, ro_sem.at[n, 0], right), remote(s_loc.at[d, j], dst_s, ro_sem.at[n, 1], right))

    def o_left(n):
        d, j, dst_o, dst_s = ((LEFT, 0, fin_o.at[1, 0], fin_s.at[1, 0]), (FAR, 1, f_o.at[1], f_s.at[1]),
                              (LEFT, 1, fin_o.at[1, 1], fin_s.at[1, 1]))[n]
        return (remote(p_loc.at[d, j], dst_o, lo_sem.at[n, 0], left), remote(s_loc.at[d, j], dst_s, lo_sem.at[n, 1], left))

    def px_copy(which, n):
        return remote(px_send.at[n], px_recv.at[which, n], px_sem.at[which, n], partner)

    def start(copies):
        for cp in copies:
            cp.start()

    def wait_recv(copies):
        for cp in copies:
            cp.wait_recv()

    def wait_send(copies):
        for cp in copies:
            cp.wait_send()

    lane = lax.broadcasted_iota(jnp.int32, (tokens, 128), 1)

    def softmax_part(qv, kk, vv, mask=None):
        s = lax.dot_general(qv, kk, (((1,), (1,)), ((), ())), preferred_element_type=F32) * score_scale
        if mask is not None:
            s = jnp.where(mask, s, NEG)
        m = jnp.max(s, axis=1, keepdims=True)
        p = jnp.exp2(s - m)
        z = jnp.sum(p, axis=1, keepdims=True)
        return jnp.dot(p.astype(BF), vv, preferred_element_type=F32), m, z

    def attend_pages(d, hb, o_ref, s_ref):
        ca = chip_of[d]

        def body(t, carry):
            j = lax.div(t, 2)
            g = lax.rem(t, 2)
            where = [idx[(CORES * ca + j) * slots + s] for s in range(slots)]
            stats = s_ref[d, j]
            for ii in range(part):
                head = hb * half + g * part + ii
                kk = jnp.concatenate([pages[w, 0, head] for w in where], axis=0)
                vv = jnp.concatenate([pages[w, 1, head] for w in where], axis=0)
                o, m, z = softmax_part(q[ca, hb, g, ii, j], kk, vv)
                o_ref[d, j, g * part + ii] = o
                stats = jnp.where(lane == g * part + ii, m, jnp.where(lane == half + g * part + ii, z, stats))
            s_ref[d, j] = stats
            return carry
        lax.fori_loop(0, 2 * CORES, body, 0)

    def attend_new():
        row = lax.broadcasted_iota(jnp.int32, (tokens, tokens), 0)
        col = lax.broadcasted_iota(jnp.int32, (tokens, tokens), 1)
        mask = col <= row

        def body(j, carry):
            stats = n_s[j]
            for i in range(half):
                o, m, z = softmax_part(q[chip, core, i // part, i % part, j], k_new[i, j], v_new[i, j], mask)
                n_o[j, i] = o
                stats = jnp.where(lane == i, m, jnp.where(lane == half + i, z, stats))
            n_s[j] = stats
            return carry
        lax.fori_loop(0, CORES, body, 0)

    def merge(ao, a_s, bo, b_s):
        sa, sb = a_s[...], b_s[...]
        m = jnp.maximum(sa, sb)
        wa, wb = jnp.exp2(sa - m), jnp.exp2(sb - m)
        z = sa * pltpu.roll(wa, half, axis=1) + sb * pltpu.roll(wb, half, axis=1)
        a_s[...] = jnp.where(lane < half, m, jnp.where(lane < 2 * half, z, 0.0))
        for i in range(half):
            ao[i] = ao[i] * wa[:, i:i + 1] + bo[i] * wb[:, i:i + 1]

    def merge_pair(d, j):
        merge(p_loc.at[d, j], s_loc.at[d, j], p_recv.at[d, j], s_recv.at[d, j])

    def norm_rows(v, gain):
        inv = lax.rsqrt(jnp.mean(v * v, axis=-1, keepdims=True) + NORM_EPS)
        return (v * inv * gain).astype(BF)

    ROWS = 16

    def norm_only(gain):
        def body(b, carry):
            r = pl.ds(pl.multiple_of(b * ROWS, ROWS), ROWS)
            h[r, :] = norm_rows(x[r, :].astype(F32), gain)
            return carry
        lax.fori_loop(0, rows // ROWS, body, 0)

    def add_norm(which, gain):
        n_col = dim // OUT_COL
        for n in range(n_col):
            px_copy(which, n).wait()

        def body(b, carry):
            r = pl.ds(pl.multiple_of(b * ROWS, ROWS), ROWS)
            total = jnp.concatenate([px_send[n, r, :] + px_recv[which, n, r, :] for n in range(n_col)], axis=1)
            xv = (x[r, :].astype(F32) + total).astype(BF)
            x[r, :] = xv
            h[r, :] = norm_rows(xv.astype(F32), gain)
            return carry
        lax.fori_loop(0, rows // ROWS, body, 0)

    def dot(a, b):
        return jnp.dot(a, b, preferred_element_type=F32)

    def qkv_pair(l, t):
        w = (wq, wk, wv)[t // 2]
        for sub in range(2):
            qkv_copy(l, t, w, sub).wait()
        hv = h[...]
        for sub in range(2):
            res = dot(hv, ring[2 * t + sub])
            for e in range(COL // hd):
                v = res[:, e * hd:(e + 1) * hd]
                if t < 4:
                    v = v * cos[...] + pltpu.roll(v, hd // 2, axis=1) * sin[...]
                v = v.astype(BF)
                i = (t % 2) * part + sub * (COL // hd) + e
                for j in range(CORES):
                    vj = v[j * tokens:(j + 1) * tokens]
                    if t < 2:
                        q[chip, core, i // part, i % part, j] = vj
                    elif t < 4:
                        k_new[i, j] = vj
                    else:
                        v_new[i, j] = vj
        for sub in range(2):
            gu_copy(l, t, sub).start()

    barrier = pltpu.get_barrier_semaphore()
    for dev in (partner, left, right):
        pl.semaphore_signal(barrier, inc=1, device_id={"pool": dev}, device_id_type=MESH)
    for t in range(PAIRS):
        start_qkv(0, t)
    for p in range(STAGE):
        page_copy(0, p).start()
    s_loc[...] = jnp.zeros_like(s_loc)
    s_send[...] = jnp.zeros_like(s_send)
    n_s[...] = jnp.zeros_like(n_s)
    own_rows = pl.ds(pl.multiple_of(core * tokens, tokens), tokens)
    x[own_rows, :] = hid[...]
    pl.semaphore_wait(barrier, 3)
    x_copy = remote(hid, x.at[own_rows], x_sem, partner)
    x_copy.start()
    for n in range(dim // OUT_COL):
        wo_copy(0, n).start()
    for n in range(dim // COL):
        wd_copy(0, n).start()
    turn_pages(0, 0, n_pages)
    x_copy.wait()
    norm_only(gain_a[0])

    def layer(l, carry):
        for t in range(2):
            qkv_pair(l, t)
        for n in range(2):
            q_right(n).start()
            q_left(n).start()
        for n in range(2):
            q_part(n).start()
        for t in range(2, 6):
            qkv_pair(l, t)
        attend_new()
        attend_pages(OWN, core, p_loc, s_loc)

        q_right(0).wait_recv()
        q_right(2).start()
        q_part(2).start()
        q_left(0).wait_recv()
        q_left(2).start()
        q_part(5).start()

        q_part(0).wait_recv()
        q_part(1).wait_recv()
        attend_pages(OWN, other, p_send, s_send)
        start(o_part(OWN))

        q_right(1).wait_recv()
        q_part(3).start()
        q_left(1).wait_recv()
        q_part(4).start()
        attend_pages(LEFT, core, p_loc, s_loc)
        attend_pages(RIGHT, core, p_loc, s_loc)
        q_part(2).wait_recv()
        q_part(3).wait_recv()
        attend_pages(LEFT, other, p_send, s_send)
        start(o_part(LEFT))
        q_right(2).wait_recv()
        q_part(6).start()
        q_left(2).wait_recv()
        q_part(7).start()
        q_part(4).wait_recv()
        q_part(5).wait_recv()
        attend_pages(RIGHT, other, p_send, s_send)
        start(o_part(RIGHT))

        wait_recv(o_part(LEFT))
        merge_pair(LEFT, 0)
        start(o_left(0))
        wait_recv(o_part(RIGHT))
        merge_pair(RIGHT, 1)
        start(o_right(0))

        q_part(6).wait_recv()
        q_part(7).wait_recv()
        attend_pages(FAR, other, p_send, s_send)
        start(o_part(FAR))
        attend_pages(FAR, core, p_loc, s_loc)
        wait_recv(o_part(FAR))
        merge_pair(FAR, 0)
        start(o_right(1))
        merge_pair(FAR, 1)
        start(o_left(1))
        merge_pair(RIGHT, 0)
        merge_pair(LEFT, 1)
        wait_recv(o_part(OWN))
        for j in range(CORES):
            merge_pair(OWN, j)
            merge(p_loc.at[OWN, j], s_loc.at[OWN, j], n_o.at[j], n_s.at[j])
        for n in range(8):
            q_part(n).wait_send()
        for n in range(3):
            q_right(n).wait_send()
            q_left(n).wait_send()
        for d in range(4):
            wait_send(o_part(d))

        @pl.when(l + 1 < layers)
        def _():
            turn_pages(l + 1, 0, n_pages // 2)

        wait_recv(o_right(1))
        merge(p_loc.at[RIGHT, 0], s_loc.at[RIGHT, 0], f_o.at[0], f_s.at[0])
        start(o_right(2))
        wait_recv(o_left(1))
        merge(p_loc.at[LEFT, 1], s_loc.at[LEFT, 1], f_o.at[1], f_s.at[1])
        start(o_left(2))

        @pl.when(l + 1 < layers)
        def _():
            turn_pages(l + 1, n_pages // 2, n_pages)

        wait_recv(o_right(0))
        merge(p_loc.at[OWN, 1], s_loc.at[OWN, 1], fin_o.at[0, 1], fin_s.at[0, 1])
        wait_recv(o_left(0))
        merge(p_loc.at[OWN, 0], s_loc.at[OWN, 0], fin_o.at[1, 0], fin_s.at[1, 0])
        wait_recv(o_right(2))
        merge(p_loc.at[OWN, 0], s_loc.at[OWN, 0], fin_o.at[0, 0], fin_s.at[0, 0])
        wait_recv(o_left(2))
        merge(p_loc.at[OWN, 1], s_loc.at[OWN, 1], fin_o.at[1, 1], fin_s.at[1, 1])
        for n in range(3):
            wait_send(o_right(n))
            wait_send(o_left(n))
        for j in range(CORES):
            inv = 1.0 / s_loc[OWN, j]
            for i in range(half):
                att[j * tokens:(j + 1) * tokens, i * hd:(i + 1) * hd] = (p_loc[OWN, j, i] * inv[:, half + i:half + i + 1]).astype(BF)

        def out_body(n, carry):
            wo_copy(l, n).wait()
            px_send[n] = dot(att[...], wo_buf[n])
            px_copy(0, n).start()

            @pl.when(l + 1 < layers)
            def _():
                wo_copy(l + 1, n).start()
            return carry
        lax.fori_loop(0, dim // OUT_COL, out_body, 0)
        add_norm(0, gain_m[l])

        def gu_body(j, carry):
            for sub in range(2):
                gu_copy(l, j, sub).wait()
            sp = lax.rem(j, PAIRS)
            hv = h[...]
            gate = dot(hv, ring[2 * sp])
            upper = dot(hv, ring[2 * sp + 1])
            val = gate / (1.0 + jnp.exp(-gate)) * upper
            col = lax.broadcasted_iota(jnp.int32, (rows, COL), 1) + j * COL
            val = jnp.where(col >= core * overlap, val, 0.0)
            inner[:, pl.ds(pl.multiple_of(j * COL, COL), COL)] = val.astype(BF)

            @pl.when(j + PAIRS < ff_chunks)
            def _():
                for sub in range(2):
                    gu_copy(l, j + PAIRS, sub).start()

            @pl.when((j + PAIRS >= ff_chunks) & (l + 1 < layers))
            def _():
                start_qkv(l + 1, sp)
            return carry
        lax.fori_loop(0, ff_chunks, gu_body, 0)

        def down_body(n, carry):
            iv = inner[...]
            for sub in range(OUT_COL // COL):
                wd_copy(l, 2 * n + sub).wait()
            for sub in range(OUT_COL // COL):
                px_send[n, :, sub * COL:(sub + 1) * COL] = dot(iv, wd_buf[2 * n + sub])
            px_copy(1, n).start()

            @pl.when(l + 1 < layers)
            def _():
                for sub in range(OUT_COL // COL):
                    wd_copy(l + 1, 2 * n + sub).start()
            return carry
        lax.fori_loop(0, dim // OUT_COL, down_body, 0)
        add_norm(1, gain_a[lax.rem(l + 1, layers)])
        return carry
    lax.fori_loop(0, layers, layer, 0)
    out[...] = x[own_rows, :]


def solution(mesh):
    group = mesh.shape["pool"]

    def local_program(kv, idx, hid, attn_norm, w_query, w_key, w_value, w_out, mlp_norm, w_gate, w_up, w_down):
        layers, n_pages, _, page_len, heads, hd = kv.shape
        slots = idx.shape[2]
        _, tokens, dim = hid.shape
        ff = w_gate.shape[2]
        half, rows = heads // CORES, CORES * tokens
        ff_cols = -(-ff // (CORES * COL)) * COL
        cosine, sine = rope_tables(group * slots * page_len, tokens, hd)
        cos2 = jnp.asarray(np.tile(cosine, (CORES, 1)))
        sin2 = jnp.asarray(np.tile(sine, (CORES, 1)))
        cfg = (layers, tokens, dim, heads, hd, ff, n_pages, slots)
        vmem = pl.BlockSpec(memory_space=pltpu.VMEM)
        hbm = pl.BlockSpec(memory_space=pl.ANY)
        smem = pl.BlockSpec(memory_space=pltpu.SMEM)
        dma = pltpu.SemaphoreType.DMA
        o_block = (half, tokens, hd)
        s_block = (tokens, 128)
        n_out = dim // OUT_COL
        scratch = [
            pltpu.VMEM((rows, dim), BF), pltpu.VMEM((rows, dim), BF), pltpu.VMEM((rows, half * hd), BF), pltpu.VMEM((rows, ff_cols), BF),
            pltpu.VMEM((CHIPS, CORES, 2, half // 2, CORES, tokens, hd), BF),
            pltpu.VMEM((half, CORES, tokens, hd), BF), pltpu.VMEM((half, CORES, tokens, hd), BF),
            pltpu.VMEM((n_pages, 2, heads, page_len, hd), BF),
            pltpu.VMEM((STAGE, 2, page_len, heads, hd), BF),
            pltpu.VMEM((2, heads * PITCH, hd), F32),
            pltpu.VMEM((4, CORES) + o_block, F32), pltpu.VMEM((4, CORES) + o_block, F32), pltpu.VMEM((4, CORES) + o_block, F32),
            pltpu.VMEM((4, CORES) + s_block, F32), pltpu.VMEM((4, CORES) + s_block, F32), pltpu.VMEM((4, CORES) + s_block, F32),
            pltpu.VMEM((CORES,) + o_block, F32), pltpu.VMEM((CORES,) + s_block, F32),
            pltpu.VMEM((2,) + o_block, F32), pltpu.VMEM((2,) + s_block, F32),
            pltpu.VMEM((2, CORES) + o_block, F32), pltpu.VMEM((2, CORES) + s_block, F32),
            pltpu.VMEM((n_out, rows, OUT_COL), F32), pltpu.VMEM((2, n_out, rows, OUT_COL), F32),
            pltpu.VMEM((2 * PAIRS, dim, COL), BF), pltpu.VMEM((n_out, half * hd, OUT_COL), BF), pltpu.VMEM((dim // COL, ff_cols, COL), BF),
            dma((2 * PAIRS,)), dma((n_out,)), dma((dim // COL,)), dma((STAGE,)),
            dma((2,)), dma((8, 2)), dma((3, 2)), dma((3, 2)), dma((4, 2, 2)), dma((3, 2, 2)), dma((3, 2, 2)), dma((2, n_out, 2)),
        ]
        result = pl.pallas_call(
            functools.partial(kernel, cfg),
            out_shape=jax.ShapeDtypeStruct((tokens, dim), BF),
            in_specs=[smem] + [vmem] * 5 + [hbm] * 8,
            out_specs=vmem,
            scratch_shapes=scratch,
            compiler_params=pltpu.CompilerParams(collective_id=0, has_side_effects=True, vmem_limit_bytes=67043328),
            name="decoder",
        )(idx.reshape(-1), hid[0], cos2, sin2, attn_norm.astype(F32)[:, None, :], mlp_norm.astype(F32)[:, None, :],
          kv, w_query, w_key, w_value, w_out, w_gate, w_up, w_down)
        return result[None]

    data_specs = (P(None, ("rep", "pool")), P(None, ("rep", "pool"), None), P(("rep", "pool")))
    return jax.shard_map(local_program, mesh=mesh, in_specs=data_specs + (P(),) * 9, out_specs=P(("rep", "pool")), check_vma=False)
```

time: 763 us -> 258 us (0.34)
  Pallas kernels: 0 us -> 250 us
  local copies, waits for them, and re-layouts: 255 us -> 5.41 us
  waiting for transfers between devices: 216 us -> 0 us
  matrix products: 203 us -> 0 us
  other arithmetic: 59.1 us -> 1.35 us
  starting transfers between devices: 21.6 us -> 0 us
    pallas_call x0 -> x1, Pallas kernels: none -> 250 us  [local_program(): pl.pallas_call(functools.partial(kernel, cfg), out_shape=jax.ShapeDtypeSt...]
    all_to_all x3 -> x0, waiting for transfers between devices: 216 us -> none  [local_program(): incoming = lax.all_to_all(outgoing, 'pool', 0, 0, tiled=True)]
    dot_general x33 -> x0, matrix products: 203 us -> none  [the longest x3 30.8 us: attend(): jnp.einsum('...thps,...pshd->...thd', prob_pre, val_pre, preferred_elemen...]
    dot_general x8 -> x0, local copies, waits for them, and re-layouts: 107 us -> none  [the longest x4 53.7 us: decoder_layer(): jnp.dot(normed, q_weight, preferred_element_type=jnp.float32)]
    select_n x3 -> x0, local copies, waits for them, and re-layouts: 40.9 us -> none  [local_program(): outgoing = jnp.take(kv_local[layer], page_rows, axis=0)]
    gather x3 -> x0, local copies, waits for them, and re-layouts: 40.3 us -> none  [local_program(): outgoing = jnp.take(kv_local[layer], page_rows, axis=0)]
    squeeze x1 -> x0, local copies, waits for them, and re-layouts: 33.1 us -> none  [local_program(): outgoing = jnp.take(kv_local[layer], page_rows, axis=0)]
    slice x3 -> x0, local copies, waits for them, and re-layouts: 32.9 us -> none  [attend(): val_pre = pages_kv[..., :, 1, :, :, :]]
  transfers between devices with their start and end apart: 3 -> 0, of which waited for: 3 -> 0; matrix products, arithmetic and copies ran while one was open for 44% -> 0% of each run, Pallas kernels for 0% -> 0%
where the time goes in v1:
time: 258 us; the launch traced here: 257 us
  Pallas kernels  250 us (97%)
  local copies, waits for them, and re-layouts  5.41 us (2%)
    pallas_call x1, Pallas kernels, local_program(): pl.pallas_call(functools.partial(kernel, cfg), out_shape=jax.ShapeDtypeSt...  250 us

profile of v1, /device:TPU:113, one launch (start us, length us, event | category | flops | bytes accessed | tf_op | source)
XLA Modules:
  0.0 257.1 jit_solution(15752162966839799491)
XLA Ops:
  0.0 0.5 broadcast.3
  0.5 1.3 reduce.3
  1.9 0.6 reshape.3.idx
  2.4 1.3 reshape.4.gain_a
  3.8 1.3 reshape.5.gain_m
  5.1 250.3 %decoder.1 = bf16[64,2048]{1,0:T(8,128)(2,1)} custom-call(s32[64]{0:T(128)} %reshape.3.idx, bf16[64,2048]{1,0:T(8,128)(2,1)} %bitcast.3, f32[128,128]{1,0:T(8,128)} %constant.4.clone.cos, f32[128,128]{1,0:T(8,128)} %constant.5.clone.sin, f32[3,1,2048]{2,1,0:T(1,128)} %reshape.4.gain_a, f32[3,1,2048]{2,1,0:T(1,128)} %reshape.5.gain_m, ...), custom_call_target="tpu_custom_call" | custom-call | tf_op jit(solution)/shard_map/decoder/pallas_call | solution.py:500
  255.4 1.7 copy.16

commit v2 on v1

--- a/solution.py
+++ b/solution.py
@@ -37,7 +37,7 @@
 def kernel(cfg, idx, hid, cos, sin, gain_a, gain_m, kv, wq, wk, wv, wo, wg, wu, wd, out,
            x, h, att, inner, q, k_new, v_new, pages, stage, unpack,
            p_loc, p_send, p_recv, s_loc, s_send, s_recv, n_o, n_s,
-           f_o, f_s, fin_o, fin_s, px_send, px_recv, ring, wo_buf, wd_buf,
+           f_o, f_s, fin_o, fin_s, px_recv, raw, ring, wo_buf, wd_buf,
            ring_sem, wo_sem, wd_sem, stage_sem,
            x_sem, qp_sem, qr_sem, ql_sem, po_sem, ro_sem, lo_sem, px_sem):
     layers, tokens, dim, heads, hd, ff, n_pages, slots = cfg
@@ -135,22 +135,32 @@
                q.at[c_right, core, 0], q.at[c_right, core, 1], q.at[c_far, core, 0], q.at[c_far, core, 1])[n]
         return remote(src, src, qp_sem.at[n], partner)
 
-    def o_part(d):
-        return (remote(p_send.at[d], p_recv.at[d], po_sem.at[d, 0], partner),
-                remote(s_send.at[d], s_recv.at[d], po_sem.at[d, 1], partner))
+    def o_part(d, j):
+        return (remote(p_send.at[d, j], p_recv.at[d, j], po_sem.at[d, j, 0], partner),
+                remote(s_send.at[d, j], s_recv.at[d, j], po_sem.at[d, j, 1], partner))
+
+    def message(d, j, dst_o, dst_s, sem, dev):
+        lo, hi = pl.ds(0, part), pl.ds(part, part)
+        return (remote(s_loc.at[d, j], dst_s, sem.at[0], dev), remote(p_loc.at[d, j, lo], dst_o.at[lo], sem.at[1], dev),
+                remote(p_loc.at[d, j, hi], dst_o.at[hi], sem.at[2], dev))
 
     def o_right(n):
         d, j, dst_o, dst_s = ((RIGHT, 1, fin_o.at[0, 1], fin_s.at[0, 1]), (FAR, 0, f_o.at[0], f_s.at[0]),
                               (RIGHT, 0, fin_o.at[0, 0], fin_s.at[0, 0]))[n]
-        return (remote(p_loc.at[d, j], dst_o, ro_sem.at[n, 0], right), remote(s_loc.at[d, j], dst_s, ro_sem.at[n, 1], right))
+        return message(d, j, dst_o, dst_s, ro_sem.at[n], right)
 
     def o_left(n):
         d, j, dst_o, dst_s = ((LEFT, 0, fin_o.at[1, 0], fin_s.at[1, 0]), (FAR, 1, f_o.at[1], f_s.at[1]),
                               (LEFT, 1, fin_o.at[1, 1], fin_s.at[1, 1]))[n]
-        return (remote(p_loc.at[d, j], dst_o, lo_sem.at[n, 0], left), remote(s_loc.at[d, j], dst_s, lo_sem.at[n, 1], left))
+        return message(d, j, dst_o, dst_s, lo_sem.at[n], left)
 
     def px_copy(which, n):
-        return remote(px_send.at[n], px_recv.at[which, n], px_sem.at[which, n], partner)
+        return remote(p_send.at[n, :, pl.ds(0, OUT_COL // hd)], px_recv.at[which, n], px_sem.at[which, n], partner)
+
+    def put_partial(n, first, v):
+        for j in range(CORES):
+            for c in range(v.shape[1] // hd):
+                p_send[n, j, first + c] = v[j * tokens:(j + 1) * tokens, c * hd:(c + 1) * hd]
 
     def start(copies):
         for cp in copies:
@@ -166,33 +176,48 @@
 
     lane = lax.broadcasted_iota(jnp.int32, (tokens, 128), 1)
 
-    def softmax_part(qv, kk, vv, mask=None):
-        s = lax.dot_general(qv, kk, (((1,), (1,)), ((), ())), preferred_element_type=F32) * score_scale
+    def attention(blocks, stats, mask=None):
+        scores = [lax.dot_general(qv, kk(), (((1,), (1,)), ((), ())), preferred_element_type=F32) for _, qv, kk, _, _ in blocks]
+        scores = [s * score_scale for s in scores]
         if mask is not None:
-            s = jnp.where(mask, s, NEG)
-        m = jnp.max(s, axis=1, keepdims=True)
-        p = jnp.exp2(s - m)
-        z = jnp.sum(p, axis=1, keepdims=True)
-        return jnp.dot(p.astype(BF), vv, preferred_element_type=F32), m, z
-
-    def attend_pages(d, hb, o_ref, s_ref):
-        ca = chip_of[d]
-
+            scores = [jnp.where(mask, s, NEG) for s in scores]
+        tops = [jnp.max(s, axis=1, keepdims=True) for s in scores]
+        probs = [jnp.exp2(s - m) for s, m in zip(scores, tops)]
+        sums = [jnp.sum(p, axis=1, keepdims=True) for p in probs]
+        probs = [p.astype(BF) for p in probs]
+        for (i, _, _, vv, store), p in zip(blocks, probs):
+            store(jnp.dot(p, vv(), preferred_element_type=F32))
+        for (i, _, _, _, _), m, z in zip(blocks, tops, sums):
+            stats = jnp.where(lane == i, m, jnp.where(lane == half + i, z, stats))
+        return stats
+
+    def attend_pages(unit, hb, o_ref, s_ref):
         def body(t, carry):
-            j = lax.div(t, 2)
-            g = lax.rem(t, 2)
-            where = [idx[(CORES * ca + j) * slots + s] for s in range(slots)]
-            stats = s_ref[d, j]
-            for ii in range(part):
-                head = hb * half + g * part + ii
-                kk = jnp.concatenate([pages[w, 0, head] for w in where], axis=0)
-                vv = jnp.concatenate([pages[w, 1, head] for w in where], axis=0)
-                o, m, z = softmax_part(q[ca, hb, g, ii, j], kk, vv)
-                o_ref[d, j, g * part + ii] = o
-                stats = jnp.where(lane == g * part + ii, m, jnp.where(lane == half + g * part + ii, z, stats))
-            s_ref[d, j] = stats
+            d, ca, j = unit(t)
+            where = [idx[CORES * ca + j, 0, s] for s in range(slots)]
+            blocks = []
+            for i in range(half):
+                def load(b, head=hb * half + i):
+                    return jnp.concatenate([pages[w, b, head] for w in where], axis=0)
+
+                def store(o, i=i):
+                    o_ref[d, j, i] = o
+                blocks.append((i, q[ca, hb, i // part, i % part, j], functools.partial(load, 0), functools.partial(load, 1), store))
+            s_ref[d, j] = attention(blocks, s_ref[d, j])
             return carry
-        lax.fori_loop(0, 2 * CORES, body, 0)
+        lax.fori_loop(0, CORES, body, 0)
+
+    def own_unit(t):
+        return OWN, chip, t
+
+    def far_unit(t):
+        return FAR, c_far, t
+
+    def near_first(t):
+        return LEFT - t, lax.rem(chip + CHIPS - 1 + 2 * t, CHIPS), t
+
+    def near_last(t):
+        return LEFT - t, lax.rem(chip + CHIPS - 1 + 2 * t, CHIPS), 1 - t
 
     def attend_new():
         row = lax.broadcasted_iota(jnp.int32, (tokens, tokens), 0)
@@ -200,53 +225,89 @@
         mask = col <= row
 
         def body(j, carry):
-            stats = n_s[j]
+            blocks = []
             for i in range(half):
-                o, m, z = softmax_part(q[chip, core, i // part, i % part, j], k_new[i, j], v_new[i, j], mask)
-                n_o[j, i] = o
-                stats = jnp.where(lane == i, m, jnp.where(lane == half + i, z, stats))
-            n_s[j] = stats
+                def store(o, i=i):
+                    n_o[j, i] = o
+                blocks.append((i, q[chip, core, i // part, i % part, j], lambda i=i: k_new[i, j], lambda i=i: v_new[i, j], store))
+            n_s[j] = attention(blocks, n_s[j], mask)
             return carry
         lax.fori_loop(0, CORES, body, 0)
 
-    def merge(ao, a_s, bo, b_s):
-        sa, sb = a_s[...], b_s[...]
+    def weights(sa, sb):
         m = jnp.maximum(sa, sb)
         wa, wb = jnp.exp2(sa - m), jnp.exp2(sb - m)
         z = sa * pltpu.roll(wa, half, axis=1) + sb * pltpu.roll(wb, half, axis=1)
-        a_s[...] = jnp.where(lane < half, m, jnp.where(lane < 2 * half, z, 0.0))
+        return wa, wb, jnp.where(lane < half, m, jnp.where(lane < 2 * half, z, 0.0))
+
+    def blend(ao, bo, wa, wb, i):
+        return ao[i] * wa[:, i:i + 1] + bo[i] * wb[:, i:i + 1]
+
+    def merge(ao, a_s, bo, b_s):
+        wa, wb, a_s[...] = weights(a_s[...], b_s[...])
         for i in range(half):
-            ao[i] = ao[i] * wa[:, i:i + 1] + bo[i] * wb[:, i:i + 1]
+            ao[i] = blend(ao, bo, wa, wb, i)
 
     def merge_pair(d, j):
+        wait_recv(o_part(d, j))
         merge(p_loc.at[d, j], s_loc.at[d, j], p_recv.at[d, j], s_recv.at[d, j])
 
-    def norm_rows(v, gain):
-        inv = lax.rsqrt(jnp.mean(v * v, axis=-1, keepdims=True) + NORM_EPS)
-        return (v * inv * gain).astype(BF)
+    def relay(copies, side, d, j, onward):
+        ao, a_s, bo = p_loc.at[d, j], s_loc.at[d, j], f_o.at[side]
+        wait_recv(copies[:2])
+        wa, wb, a_s[...] = weights(a_s[...], f_s[side])
+        for i in range(part):
+            ao[i] = blend(ao, bo, wa, wb, i)
+        start(onward[:2])
+        wait_recv(copies[2:])
+        for i in range(part, half):
+            ao[i] = blend(ao, bo, wa, wb, i)
+        start(onward[2:])
+
+    def finish(copies, side, j):
+        ao, bo = p_loc.at[OWN, j], fin_o.at[side, j]
+        wait_recv(copies[:2])
+        wa, wb, st = weights(s_loc[OWN, j], fin_s[side, j])
+        inv = 1.0 / st
+        for i in range(half):
+            if i == part:
+                wait_recv(copies[2:])
+            o = blend(ao, bo, wa, wb, i) * inv[:, half + i:half + i + 1]
+            att[j * tokens:(j + 1) * tokens, i * hd:(i + 1) * hd] = o.astype(BF)
 
     ROWS = 16
+    n_col = dim // OUT_COL
+
+    def normalise(squares, gain):
+        inv = lax.rsqrt(jnp.sum(squares, axis=1, keepdims=True) * (1.0 / dim) + NORM_EPS)
+        for r in range(0, rows, ROWS):
+            h[r:r + ROWS, :] = (x[r:r + ROWS, :].astype(F32) * inv[r:r + ROWS] * gain).astype(BF)
+
+    def square_tiles(v):
+        v = v * v
+        return sum(v[:, c:c + 128] for c in range(0, v.shape[1], 128))
+
+    def gain_row(ref, l):
+        g = ref[0:1, :].astype(F32)
+        for n in range(1, layers):
+            g = jnp.where(l == n, ref[n:n + 1, :].astype(F32), g)
+        return g
 
     def norm_only(gain):
-        def body(b, carry):
-            r = pl.ds(pl.multiple_of(b * ROWS, ROWS), ROWS)
-            h[r, :] = norm_rows(x[r, :].astype(F32), gain)
-            return carry
-        lax.fori_loop(0, rows // ROWS, body, 0)
+        normalise(square_tiles(x[...].astype(F32)), gain)
 
     def add_norm(which, gain):
-        n_col = dim // OUT_COL
+        squares = jnp.zeros((rows, 128), F32)
         for n in range(n_col):
             px_copy(which, n).wait()
-
-        def body(b, carry):
-            r = pl.ds(pl.multiple_of(b * ROWS, ROWS), ROWS)
-            total = jnp.concatenate([px_send[n, r, :] + px_recv[which, n, r, :] for n in range(n_col)], axis=1)
-            xv = (x[r, :].astype(F32) + total).astype(BF)
-            x[r, :] = xv
-            h[r, :] = norm_rows(xv.astype(F32), gain)
-            return carry
-        lax.fori_loop(0, rows // ROWS, body, 0)
+            for c in range(OUT_COL // hd):
+                cols = slice(n * OUT_COL + c * hd, n * OUT_COL + (c + 1) * hd)
+                total = jnp.concatenate([p_send[n, j, c] + px_recv[which, n, j, c] for j in range(CORES)], axis=0)
+                xv = (x[:, cols].astype(F32) + total).astype(BF)
+                x[:, cols] = xv
+                xv = xv.astype(F32)
+                squares = squares + xv * xv
+        normalise(squares, gain)
 
     def dot(a, b):
         return jnp.dot(a, b, preferred_element_type=F32)
@@ -272,9 +333,6 @@
                         k_new[i, j] = vj
                     else:
                         v_new[i, j] = vj
-        for sub in range(2):
-            gu_copy(l, t, sub).start()
-
     barrier = pltpu.get_barrier_semaphore()
     for dev in (partner, left, right):
         pl.semaphore_signal(barrier, inc=1, device_id={"pool": dev}, device_id_type=MESH)
@@ -286,17 +344,13 @@
     s_send[...] = jnp.zeros_like(s_send)
     n_s[...] = jnp.zeros_like(n_s)
     own_rows = pl.ds(pl.multiple_of(core * tokens, tokens), tokens)
-    x[own_rows, :] = hid[...]
+    x[own_rows, :] = hid[0]
     pl.semaphore_wait(barrier, 3)
-    x_copy = remote(hid, x.at[own_rows], x_sem, partner)
+    x_copy = remote(hid.at[0], x.at[own_rows], x_sem, partner)
     x_copy.start()
-    for n in range(dim // OUT_COL):
-        wo_copy(0, n).start()
-    for n in range(dim // COL):
-        wd_copy(0, n).start()
-    turn_pages(0, 0, n_pages)
+    raw[...] = jnp.zeros_like(raw)
     x_copy.wait()
-    norm_only(gain_a[0])
+    norm_only(gain_row(gain_a, 0))
 
     def layer(l, carry):
         for t in range(2):
@@ -308,113 +362,109 @@
             q_part(n).start()
         for t in range(2, 6):
             qkv_pair(l, t)
+
+        @pl.when(l == 0)
+        def _():
+            turn_pages(0, 0, n_pages)
         attend_new()
-        attend_pages(OWN, core, p_loc, s_loc)
-
         q_right(0).wait_recv()
         q_right(2).start()
         q_part(2).start()
         q_left(0).wait_recv()
         q_left(2).start()
         q_part(5).start()
-
-        q_part(0).wait_recv()
-        q_part(1).wait_recv()
-        attend_pages(OWN, other, p_send, s_send)
-        start(o_part(OWN))
-
+        attend_pages(own_unit, core, p_loc, s_loc)
         q_right(1).wait_recv()
         q_part(3).start()
         q_left(1).wait_recv()
         q_part(4).start()
-        attend_pages(LEFT, core, p_loc, s_loc)
-        attend_pages(RIGHT, core, p_loc, s_loc)
-        q_part(2).wait_recv()
-        q_part(3).wait_recv()
-        attend_pages(LEFT, other, p_send, s_send)
-        start(o_part(LEFT))
+        for n in range(n_col):
+            wo_copy(l, n).start()
+        for t in range(PAIRS):
+            for sub in range(2):
+                gu_copy(l, t, sub).start()
+        attend_pages(near_first, core, p_loc, s_loc)
+        for n in range(2, 6):
+            q_part(n).wait_recv()
+        attend_pages(near_first, other, p_send, s_send)
+        start(o_part(LEFT, 0))
+        start(o_part(RIGHT, 1))
         q_right(2).wait_recv()
         q_part(6).start()
         q_left(2).wait_recv()
         q_part(7).start()
-        q_part(4).wait_recv()
-        q_part(5).wait_recv()
-        attend_pages(RIGHT, other, p_send, s_send)
-        start(o_part(RIGHT))
-
-        wait_recv(o_part(LEFT))
+        attend_pages(far_unit, core, p_loc, s_loc)
         merge_pair(LEFT, 0)
         start(o_left(0))
-        wait_recv(o_part(RIGHT))
         merge_pair(RIGHT, 1)
         start(o_right(0))
-
         q_part(6).wait_recv()
         q_part(7).wait_recv()
-        attend_pages(FAR, other, p_send, s_send)
-        start(o_part(FAR))
-        attend_pages(FAR, core, p_loc, s_loc)
-        wait_recv(o_part(FAR))
+        attend_pages(far_unit, other, p_send, s_send)
+        start(o_part(FAR, 0))
+        start(o_part(FAR, 1))
+        for n in range(dim // COL):
+            wd_copy(l, n).start()
+        attend_pages(near_last, core, p_loc, s_loc)
         merge_pair(FAR, 0)
         start(o_right(1))
         merge_pair(FAR, 1)
         start(o_left(1))
+        attend_pages(near_last, other, p_send, s_send)
+        start(o_part(LEFT, 1))
+        start(o_part(RIGHT, 0))
+        q_part(0).wait_recv()
+        q_part(1).wait_recv()
+        attend_pages(own_unit, other, p_send, s_send)
+        start(o_part(OWN, 0))
+        start(o_part(OWN, 1))
         merge_pair(RIGHT, 0)
         merge_pair(LEFT, 1)
-        wait_recv(o_part(OWN))
-        for j in range(CORES):
-            merge_pair(OWN, j)
-            merge(p_loc.at[OWN, j], s_loc.at[OWN, j], n_o.at[j], n_s.at[j])
         for n in range(8):
             q_part(n).wait_send()
         for n in range(3):
             q_right(n).wait_send()
             q_left(n).wait_send()
-        for d in range(4):
-            wait_send(o_part(d))
+        for j in range(CORES):
+            merge_pair(OWN, j)
+            merge(p_loc.at[OWN, j], s_loc.at[OWN, j], n_o.at[j], n_s.at[j])
 
         @pl.when(l + 1 < layers)
         def _():
             turn_pages(l + 1, 0, n_pages // 2)
-
-        wait_recv(o_right(1))
-        merge(p_loc.at[RIGHT, 0], s_loc.at[RIGHT, 0], f_o.at[0], f_s.at[0])
-        start(o_right(2))
-        wait_recv(o_left(1))
-        merge(p_loc.at[LEFT, 1], s_loc.at[LEFT, 1], f_o.at[1], f_s.at[1])
-        start(o_left(2))
-
-        @pl.when(l + 1 < layers)
-        def _():
-            turn_pages(l + 1, n_pages // 2, n_pages)
-
+        relay(o_right(1), 0, RIGHT, 0, o_right(2))
+        relay(o_left(1), 1, LEFT, 1, o_left(2))
         wait_recv(o_right(0))
         merge(p_loc.at[OWN, 1], s_loc.at[OWN, 1], fin_o.at[0, 1], fin_s.at[0, 1])
         wait_recv(o_left(0))
         merge(p_loc.at[OWN, 0], s_loc.at[OWN, 0], fin_o.at[1, 0], fin_s.at[1, 0])
-        wait_recv(o_right(2))
-        merge(p_loc.at[OWN, 0], s_loc.at[OWN, 0], fin_o.at[0, 0], fin_s.at[0, 0])
-        wait_recv(o_left(2))
-        merge(p_loc.at[OWN, 1], s_loc.at[OWN, 1], fin_o.at[1, 1], fin_s.at[1, 1])
+
+        @pl.when(l + 1 < layers)
+        def _():
+            turn_pages(l + 1, n_pages // 2, n_pages)
+        finish(o_right(2), 0, 0)
+        finish(o_left(2), 1, 1)
         for n in range(3):
             wait_send(o_right(n))
             wait_send(o_left(n))
-        for j in range(CORES):
-            inv = 1.0 / s_loc[OWN, j]
-            for i in range(half):
-                att[j * tokens:(j + 1) * tokens, i * hd:(i + 1) * hd] = (p_loc[OWN, j, i] * inv[:, half + i:half + i + 1]).astype(BF)
+        for d in range(4):
+            for j in range(CORES):
+                wait_send(o_part(d, j))
 
         def out_body(n, carry):
             wo_copy(l, n).wait()
-            px_send[n] = dot(att[...], wo_buf[n])
+            put_partial(n, 0, dot(att[...], wo_buf[n]))
             px_copy(0, n).start()
-
-            @pl.when(l + 1 < layers)
-            def _():
-                wo_copy(l + 1, n).start()
             return carry
         lax.fori_loop(0, dim // OUT_COL, out_body, 0)
-        add_norm(0, gain_m[l])
+        add_norm(0, gain_row(gain_m, l))
+
+        def gate_block(j):
+            gate, upper = raw[0], raw[1]
+            val = gate / (1.0 + jnp.exp(-gate)) * upper
+            col = lax.broadcasted_iota(jnp.int32, (rows, COL), 1) + j * COL
+            val = jnp.where(col >= core * overlap, val, 0.0)
+            inner[:, pl.ds(pl.multiple_of(j * COL, COL), COL)] = val.astype(BF)
 
         def gu_body(j, carry):
             for sub in range(2):
@@ -423,10 +473,9 @@
             hv = h[...]
             gate = dot(hv, ring[2 * sp])
             upper = dot(hv, ring[2 * sp + 1])
-            val = gate / (1.0 + jnp.exp(-gate)) * upper
-            col = lax.broadcasted_iota(jnp.int32, (rows, COL), 1) + j * COL
-            val = jnp.where(col >= core * overlap, val, 0.0)
-            inner[:, pl.ds(pl.multiple_of(j * COL, COL), COL)] = val.astype(BF)
+            gate_block(jnp.maximum(j - 1, 0))
+            raw[0] = gate
+            raw[1] = upper
 
             @pl.when(j + PAIRS < ff_chunks)
             def _():
@@ -438,25 +487,21 @@
                 start_qkv(l + 1, sp)
             return carry
         lax.fori_loop(0, ff_chunks, gu_body, 0)
+        gate_block(ff_chunks - 1)
 
         def down_body(n, carry):
             iv = inner[...]
             for sub in range(OUT_COL // COL):
                 wd_copy(l, 2 * n + sub).wait()
             for sub in range(OUT_COL // COL):
-                px_send[n, :, sub * COL:(sub + 1) * COL] = dot(iv, wd_buf[2 * n + sub])
+                put_partial(n, sub * (COL // hd), dot(iv, wd_buf[2 * n + sub]))
             px_copy(1, n).start()
-
-            @pl.when(l + 1 < layers)
-            def _():
-                for sub in range(OUT_COL // COL):
-                    wd_copy(l + 1, 2 * n + sub).start()
             return carry
         lax.fori_loop(0, dim // OUT_COL, down_body, 0)
-        add_norm(1, gain_a[lax.rem(l + 1, layers)])
+        add_norm(1, gain_row(gain_a, lax.rem(l + 1, layers)))
         return carry
     lax.fori_loop(0, layers, layer, 0)
-    out[...] = x[own_rows, :]
+    out[0] = x[own_rows, :]
 
 
 def solution(mesh):
@@ -492,22 +537,22 @@
             pltpu.VMEM((CORES,) + o_block, F32), pltpu.VMEM((CORES,) + s_block, F32),
             pltpu.VMEM((2,) + o_block, F32), pltpu.VMEM((2,) + s_block, F32),
             pltpu.VMEM((2, CORES) + o_block, F32), pltpu.VMEM((2, CORES) + s_block, F32),
-            pltpu.VMEM((n_out, rows, OUT_COL), F32), pltpu.VMEM((2, n_out, rows, OUT_COL), F32),
+            pltpu.VMEM((2, n_out, CORES, OUT_COL // hd, tokens, hd), F32), pltpu.VMEM((2, rows, COL), F32),
             pltpu.VMEM((2 * PAIRS, dim, COL), BF), pltpu.VMEM((n_out, half * hd, OUT_COL), BF), pltpu.VMEM((dim // COL, ff_cols, COL), BF),
             dma((2 * PAIRS,)), dma((n_out,)), dma((dim // COL,)), dma((STAGE,)),
-            dma((2,)), dma((8, 2)), dma((3, 2)), dma((3, 2)), dma((4, 2, 2)), dma((3, 2, 2)), dma((3, 2, 2)), dma((2, n_out, 2)),
+            dma((2,)), dma((8, 2)), dma((3, 2)), dma((3, 2)), dma((4, CORES, 2, 2)), dma((3, 3, 2)), dma((3, 3, 2)), dma((2, n_out, 2)),
         ]
         result = pl.pallas_call(
             functools.partial(kernel, cfg),
-            out_shape=jax.ShapeDtypeStruct((tokens, dim), BF),
+            out_shape=jax.ShapeDtypeStruct((1, tokens, dim), BF),
             in_specs=[smem] + [vmem] * 5 + [hbm] * 8,
             out_specs=vmem,
             scratch_shapes=scratch,
             compiler_params=pltpu.CompilerParams(collective_id=0, has_side_effects=True, vmem_limit_bytes=67043328),
             name="decoder",
-        )(idx.reshape(-1), hid[0], cos2, sin2, attn_norm.astype(F32)[:, None, :], mlp_norm.astype(F32)[:, None, :],
+        )(idx, hid, cos2, sin2, attn_norm, mlp_norm,
           kv, w_query, w_key, w_value, w_out, w_gate, w_up, w_down)
-        return result[None]
+        return result
 
     data_specs = (P(None, ("rep", "pool")), P(None, ("rep", "pool"), None), P(("rep", "pool")))
     return jax.shard_map(local_program, mesh=mesh, in_specs=data_specs + (P(),) * 9, out_specs=P(("rep", "pool")), check_vma=False)

time: 258 us -> 163 us (0.63)
  Pallas kernels: 250 us -> 161 us
  local copies, waits for them, and re-layouts: 5.41 us -> 1.67 us
    pallas_call x1, Pallas kernels: 250 us -> 161 us  [local_program(): pl.pallas_call(functools.partial(kernel, cfg), out_shape=jax.ShapeDtypeSt...]
    broadcast_in_dim x2 -> x0, local copies, waits for them, and re-layouts: 2.67 us -> none  [the longest x1 1.34 us: local_program(): attn_norm.astype(F32)[:, None, :]]
where the time goes in v2:
time: 163 us
  Pallas kernels  161 us (99%)
  local copies, waits for them, and re-layouts  1.67 us (1%)
    pallas_call x1, Pallas kernels, local_program(): pl.pallas_call(functools.partial(kernel, cfg), out_shape=jax.ShapeDtypeSt...  161 us

profile of v2, /device:TPU:113, one launch (start us, length us, event | category | flops | bytes accessed | tf_op | source)
XLA Modules:
  0.0 162.8 jit_solution(14643424038602200918)
XLA Ops:
  0.0 161.1 %decoder.1 = bf16[1,64,2048]{2,1,0:T(8,128)(2,1)} custom-call(s32[8,1,8]{2,1,0:T(1,128)} %idx.1, bf16[1,64,2048]{2,1,0:T(8,128)(2,1)} %hid.1, f32[128,128]{1,0:T(8,128)} %constant.4.clone.cos, f32[128,128]{1,0:T(8,128)} %constant.5.clone.sin, bf16[3,2048]{1,0:T(4,128)(2,1)} %gain_a.1, bf16[3,2048]{1,0:T(4,128)(2,1)} %gain_m.1, ...), custom_call_target="tpu_custom_call" | custom-call | tf_op jit(solution)/shard_map/decoder/pallas_call | solution.py:545
  161.1 1.7 %copy.16 = bf16[1,64,2048]{2,1,0:T(8,128)(2,1)} copy(bf16[1,64,2048]{2,1,0:T(8,128)(2,1)} %decoder.1) | data formatting | bytes 524288

commit v3 on v2

--- a/solution.py
+++ b/solution.py
@@ -20,9 +20,10 @@
 CHIPS = 4
 COL = 256
 PAIRS = 6
-STAGE = 8
+TURN = 2
 PITCH = 36
 OUT_COL = 512
+GATE_WAIT = 1
 
 
 def rope_tables(offset, tokens, head_dim):
@@ -35,10 +36,10 @@
 
 
 def kernel(cfg, idx, hid, cos, sin, gain_a, gain_m, kv, wq, wk, wv, wo, wg, wu, wd, out,
-           x, h, att, inner, q, k_new, v_new, pages, stage, unpack,
-           p_loc, p_send, p_recv, s_loc, s_send, s_recv, n_o, n_s,
+           x, h, att, inner, q, k_new, v_new, pages, unpack,
+           p_loc, p_send, p_recv, s_loc, s_send, s_recv, t_loc, n_o, n_s,
            f_o, f_s, fin_o, fin_s, px_recv, raw, ring, wo_buf, wd_buf,
-           ring_sem, wo_sem, wd_sem, stage_sem,
+           ring_sem, wo_sem, wd_sem, page_sem,
            x_sem, qp_sem, qr_sem, ql_sem, po_sem, ro_sem, lo_sem, px_sem):
     layers, tokens, dim, heads, hd, ff, n_pages, slots = cfg
     group = CORES * CHIPS
@@ -94,33 +95,31 @@
         return pltpu.make_async_copy(wd.at[l, pl.ds(row, ff_cols), pl.ds(pl.multiple_of(n * COL, COL), COL)],
                                      wd_buf.at[n], wd_sem.at[n])
 
-    page_len = kv.shape[3]
+    page_len = kv.shape[3] // heads
 
     def page_copy(l, p):
-        s = lax.rem(p, STAGE)
-        return pltpu.make_async_copy(kv.at[l, p], stage.at[s], stage_sem.at[s])
+        return pltpu.make_async_copy(kv.at[l, p], pages.at[p], page_sem.at[p])
+
+    def start_pages(l):
+        def body(p, carry):
+            page_copy(l, p).start()
+            return carry
+        lax.fori_loop(0, n_pages, body, 0)
 
     def turn_pages(l, lo, hi):
-        def body(p, carry):
-            page_copy(l, p).wait()
-            s = lax.rem(p, STAGE)
-            for b in range(2):
-                for r in range(page_len):
-                    unpack[b, pl.ds(r, heads, stride=PITCH), :] = stage[s, b, r].astype(F32)
-            for b in range(2):
-                for i in range(heads):
-                    pages[p, b, i] = unpack[b, pl.ds(i * PITCH, page_len), :].astype(BF)
-            nxt = p + STAGE
-
-            @pl.when(nxt < n_pages)
-            def _():
-                page_copy(l, nxt).start()
-
-            @pl.when((nxt >= n_pages) & (l + 1 < layers))
-            def _():
-                page_copy(l + 1, nxt - n_pages).start()
+        def body(t, carry):
+            for e in range(TURN):
+                page_copy(l, TURN * t + e).wait()
+            for e in range(TURN):
+                for b in range(2):
+                    for r in range(page_len):
+                        unpack[e, b, pl.ds(r, heads, stride=PITCH), :] = pages[TURN * t + e, b, r * heads:(r + 1) * heads].astype(F32)
+            for e in range(TURN):
+                for b in range(2):
+                    for i in range(heads):
+                        pages[TURN * t + e, b, i * page_len:(i + 1) * page_len] = unpack[e, b, pl.ds(i * PITCH, page_len), :].astype(BF)
             return carry
-        lax.fori_loop(lo, hi, body, 0)
+        lax.fori_loop(lo // TURN, hi // TURN, body, 0)
 
     def q_right(n):
         src = (q.at[chip, core, 0], q.at[chip, core, 1], q.at[c_left, core, 0])[n]
@@ -141,7 +140,7 @@
 
     def message(d, j, dst_o, dst_s, sem, dev):
         lo, hi = pl.ds(0, part), pl.ds(part, part)
-        return (remote(s_loc.at[d, j], dst_s, sem.at[0], dev), remote(p_loc.at[d, j, lo], dst_o.at[lo], sem.at[1], dev),
+        return (remote(t_loc.at[d, j], dst_s, sem.at[0], dev), remote(p_loc.at[d, j, lo], dst_o.at[lo], sem.at[1], dev),
                 remote(p_loc.at[d, j, hi], dst_o.at[hi], sem.at[2], dev))
 
     def o_right(n):
@@ -198,11 +197,11 @@
             blocks = []
             for i in range(half):
                 def load(b, head=hb * half + i):
-                    return jnp.concatenate([pages[w, b, head] for w in where], axis=0)
+                    return jnp.concatenate([pages[w, b, pl.ds(pl.multiple_of(head * page_len, page_len), page_len)] for w in where], axis=0)
 
                 def store(o, i=i):
                     o_ref[d, j, i] = o
-                blocks.append((i, q[ca, hb, i // part, i % part, j], functools.partial(load, 0), functools.partial(load, 1), store))
+                blocks.append((i, q[ca, hb, j, i], functools.partial(load, 0), functools.partial(load, 1), store))
             s_ref[d, j] = attention(blocks, s_ref[d, j])
             return carry
         lax.fori_loop(0, CORES, body, 0)
@@ -229,7 +228,7 @@
             for i in range(half):
                 def store(o, i=i):
                     n_o[j, i] = o
-                blocks.append((i, q[chip, core, i // part, i % part, j], lambda i=i: k_new[i, j], lambda i=i: v_new[i, j], store))
+                blocks.append((i, q[chip, core, j, i], lambda i=i: k_new[i, j], lambda i=i: v_new[i, j], store))
             n_s[j] = attention(blocks, n_s[j], mask)
             return carry
         lax.fori_loop(0, CORES, body, 0)
@@ -243,37 +242,53 @@
     def blend(ao, bo, wa, wb, i):
         return ao[i] * wa[:, i:i + 1] + bo[i] * wb[:, i:i + 1]
 
-    def merge(ao, a_s, bo, b_s):
-        wa, wb, a_s[...] = weights(a_s[...], b_s[...])
+    def merge(ao, a_s, bo, sb):
+        wa, wb, a_s[...] = weights(a_s[...], sb)
         for i in range(half):
             ao[i] = blend(ao, bo, wa, wb, i)
 
+    def pack(v):
+        out_v = v[0:8]
+        for r in range(1, tokens // 8):
+            out_v = out_v + pltpu.roll(v[8 * r:8 * r + 8], 2 * half * r, axis=1)
+        return out_v
+
+    def unpacked(v):
+        blocks = [v] + [pltpu.roll(v, 128 - 2 * half * r, axis=1) for r in range(1, tokens // 8)]
+        return jnp.where(lane < 2 * half, jnp.concatenate(blocks, axis=0), 0.0)
+
+    def send(d, j, copies):
+        t_loc[d, j] = pack(s_loc[d, j])
+        start(copies)
+
     def merge_pair(d, j):
         wait_recv(o_part(d, j))
-        merge(p_loc.at[d, j], s_loc.at[d, j], p_recv.at[d, j], s_recv.at[d, j])
-
-    def relay(copies, side, d, j, onward):
-        ao, a_s, bo = p_loc.at[d, j], s_loc.at[d, j], f_o.at[side]
+        merge(p_loc.at[d, j], s_loc.at[d, j], p_recv.at[d, j], s_recv[d, j])
+
+    def relay_first(copies, side, d, j, onward):
         wait_recv(copies[:2])
-        wa, wb, a_s[...] = weights(a_s[...], f_s[side])
+        wa, wb, s_loc[d, j] = weights(s_loc[d, j], unpacked(f_s[side]))
         for i in range(part):
-            ao[i] = blend(ao, bo, wa, wb, i)
-        start(onward[:2])
+            p_loc[d, j, i] = blend(p_loc.at[d, j], f_o.at[side], wa, wb, i)
+        send(d, j, onward[:2])
+        return wa, wb
+
+    def relay_last(copies, side, d, j, onward, scales):
         wait_recv(copies[2:])
         for i in range(part, half):
-            ao[i] = blend(ao, bo, wa, wb, i)
+            p_loc[d, j, i] = blend(p_loc.at[d, j], f_o.at[side], *scales, i)
         start(onward[2:])
 
-    def finish(copies, side, j):
-        ao, bo = p_loc.at[OWN, j], fin_o.at[side, j]
-        wait_recv(copies[:2])
-        wa, wb, st = weights(s_loc[OWN, j], fin_s[side, j])
-        inv = 1.0 / st
-        for i in range(half):
-            if i == part:
-                wait_recv(copies[2:])
-            o = blend(ao, bo, wa, wb, i) * inv[:, half + i:half + i + 1]
+    def finish(ready, side, j, lo, hi, scales=None):
+        wait_recv(ready)
+        if scales is None:
+            wa, wb, st = weights(s_loc[OWN, j], unpacked(fin_s[side, j]))
+            scales = (wa, wb, 1.0 / st)
+        wa, wb, inv = scales
+        for i in range(lo, hi):
+            o = blend(p_loc.at[OWN, j], fin_o.at[side, j], wa, wb, i) * inv[:, half + i:half + i + 1]
             att[j * tokens:(j + 1) * tokens, i * hd:(i + 1) * hd] = o.astype(BF)
+        return scales
 
     ROWS = 16
     n_col = dim // OUT_COL
@@ -312,10 +327,12 @@
     def dot(a, b):
         return jnp.dot(a, b, preferred_element_type=F32)
 
+    def wait_qkv(l, lo, hi):
+        for t in range(lo, hi):
+            for sub in range(2):
+                qkv_copy(l, t, (wq, wk, wv)[t // 2], sub).wait()
+
     def qkv_pair(l, t):
-        w = (wq, wk, wv)[t // 2]
-        for sub in range(2):
-            qkv_copy(l, t, w, sub).wait()
         hv = h[...]
         for sub in range(2):
             res = dot(hv, ring[2 * t + sub])
@@ -328,7 +345,7 @@
                 for j in range(CORES):
                     vj = v[j * tokens:(j + 1) * tokens]
                     if t < 2:
-                        q[chip, core, i // part, i % part, j] = vj
+                        q[chip, core, j, i] = vj
                     elif t < 4:
                         k_new[i, j] = vj
                     else:
@@ -338,8 +355,7 @@
         pl.semaphore_signal(barrier, inc=1, device_id={"pool": dev}, device_id_type=MESH)
     for t in range(PAIRS):
         start_qkv(0, t)
-    for p in range(STAGE):
-        page_copy(0, p).start()
+    start_pages(0)
     s_loc[...] = jnp.zeros_like(s_loc)
     s_send[...] = jnp.zeros_like(s_send)
     n_s[...] = jnp.zeros_like(n_s)
@@ -353,6 +369,7 @@
     norm_only(gain_row(gain_a, 0))
 
     def layer(l, carry):
+        wait_qkv(l, 0, 2)
         for t in range(2):
             qkv_pair(l, t)
         for n in range(2):
@@ -360,12 +377,14 @@
             q_left(n).start()
         for n in range(2):
             q_part(n).start()
+        wait_qkv(l, 2, 6)
         for t in range(2, 6):
             qkv_pair(l, t)
 
         @pl.when(l == 0)
         def _():
             turn_pages(0, 0, n_pages)
+        attend_pages(own_unit, core, p_loc, s_loc)
         attend_new()
         q_right(0).wait_recv()
         q_right(2).start()
@@ -373,51 +392,54 @@
         q_left(0).wait_recv()
         q_left(2).start()
         q_part(5).start()
-        attend_pages(own_unit, core, p_loc, s_loc)
+        attend_pages(near_first, core, p_loc, s_loc)
+        q_part(2).wait_recv()
+        q_part(5).wait_recv()
+        attend_pages(near_first, other, p_send, s_send)
+        start(o_part(LEFT, 0))
+        start(o_part(RIGHT, 1))
         q_right(1).wait_recv()
         q_part(3).start()
         q_left(1).wait_recv()
         q_part(4).start()
+        attend_pages(near_last, core, p_loc, s_loc)
+        merge_pair(LEFT, 0)
+        send(LEFT, 0, o_left(0))
+        merge_pair(RIGHT, 1)
+        send(RIGHT, 1, o_right(0))
+        q_part(3).wait_recv()
+        q_part(4).wait_recv()
         for n in range(n_col):
             wo_copy(l, n).start()
         for t in range(PAIRS):
             for sub in range(2):
                 gu_copy(l, t, sub).start()
-        attend_pages(near_first, core, p_loc, s_loc)
-        for n in range(2, 6):
-            q_part(n).wait_recv()
-        attend_pages(near_first, other, p_send, s_send)
-        start(o_part(LEFT, 0))
-        start(o_part(RIGHT, 1))
+        attend_pages(near_last, other, p_send, s_send)
+        start(o_part(LEFT, 1))
+        start(o_part(RIGHT, 0))
         q_right(2).wait_recv()
         q_part(6).start()
         q_left(2).wait_recv()
         q_part(7).start()
         attend_pages(far_unit, core, p_loc, s_loc)
-        merge_pair(LEFT, 0)
-        start(o_left(0))
-        merge_pair(RIGHT, 1)
-        start(o_right(0))
         q_part(6).wait_recv()
         q_part(7).wait_recv()
         attend_pages(far_unit, other, p_send, s_send)
         start(o_part(FAR, 0))
         start(o_part(FAR, 1))
-        for n in range(dim // COL):
-            wd_copy(l, n).start()
-        attend_pages(near_last, core, p_loc, s_loc)
-        merge_pair(FAR, 0)
-        start(o_right(1))
-        merge_pair(FAR, 1)
-        start(o_left(1))
-        attend_pages(near_last, other, p_send, s_send)
-        start(o_part(LEFT, 1))
-        start(o_part(RIGHT, 0))
         q_part(0).wait_recv()
         q_part(1).wait_recv()
         attend_pages(own_unit, other, p_send, s_send)
         start(o_part(OWN, 0))
         start(o_part(OWN, 1))
+        merge_pair(FAR, 0)
+        send(FAR, 0, o_right(1))
+        merge_pair(FAR, 1)
+        send(FAR, 1, o_left(1))
+
+        @pl.when(l + 1 < layers)
+        def _():
+            start_pages(l + 1)
         merge_pair(RIGHT, 0)
         merge_pair(LEFT, 1)
         for n in range(8):
@@ -427,23 +449,29 @@
             q_left(n).wait_send()
         for j in range(CORES):
             merge_pair(OWN, j)
-            merge(p_loc.at[OWN, j], s_loc.at[OWN, j], n_o.at[j], n_s.at[j])
+            merge(p_loc.at[OWN, j], s_loc.at[OWN, j], n_o.at[j], n_s[j])
 
         @pl.when(l + 1 < layers)
         def _():
             turn_pages(l + 1, 0, n_pages // 2)
-        relay(o_right(1), 0, RIGHT, 0, o_right(2))
-        relay(o_left(1), 1, LEFT, 1, o_left(2))
+        from_left = relay_first(o_right(1), 0, RIGHT, 0, o_right(2))
+        from_right = relay_first(o_left(1), 1, LEFT, 1, o_left(2))
+        relay_last(o_right(1), 0, RIGHT, 0, o_right(2), from_left)
+        relay_last(o_left(1), 1, LEFT, 1, o_left(2), from_right)
+        for n in range(dim // COL):
+            wd_copy(l, n).start()
         wait_recv(o_right(0))
-        merge(p_loc.at[OWN, 1], s_loc.at[OWN, 1], fin_o.at[0, 1], fin_s.at[0, 1])
+        merge(p_loc.at[OWN, 1], s_loc.at[OWN, 1], fin_o.at[0, 1], unpacked(fin_s[0, 1]))
         wait_recv(o_left(0))
-        merge(p_loc.at[OWN, 0], s_loc.at[OWN, 0], fin_o.at[1, 0], fin_s.at[1, 0])
+        merge(p_loc.at[OWN, 0], s_loc.at[OWN, 0], fin_o.at[1, 0], unpacked(fin_s[1, 0]))
 
         @pl.when(l + 1 < layers)
         def _():
             turn_pages(l + 1, n_pages // 2, n_pages)
-        finish(o_right(2), 0, 0)
-        finish(o_left(2), 1, 1)
+        first = finish(o_right(2)[:2], 0, 0, 0, part)
+        second = finish(o_left(2)[:2], 1, 1, 0, part)
+        finish(o_right(2)[2:], 0, 0, part, half, first)
+        finish(o_left(2)[2:], 1, 1, part, half, second)
         for n in range(3):
             wait_send(o_right(n))
             wait_send(o_left(n))
@@ -451,53 +479,51 @@
             for j in range(CORES):
                 wait_send(o_part(d, j))
 
-        def out_body(n, carry):
+        for n in range(n_col):
             wo_copy(l, n).wait()
+        for n in range(n_col):
             put_partial(n, 0, dot(att[...], wo_buf[n]))
             px_copy(0, n).start()
-            return carry
-        lax.fori_loop(0, dim // OUT_COL, out_body, 0)
         add_norm(0, gain_row(gain_m, l))
 
         def gate_block(j):
             gate, upper = raw[0], raw[1]
             val = gate / (1.0 + jnp.exp(-gate)) * upper
-            col = lax.broadcasted_iota(jnp.int32, (rows, COL), 1) + j * COL
-            val = jnp.where(col >= core * overlap, val, 0.0)
-            inner[:, pl.ds(pl.multiple_of(j * COL, COL), COL)] = val.astype(BF)
-
-        def gu_body(j, carry):
-            for sub in range(2):
-                gu_copy(l, j, sub).wait()
-            sp = lax.rem(j, PAIRS)
+            if j * COL < overlap:
+                col = lax.broadcasted_iota(jnp.int32, (rows, COL), 1) + j * COL
+                val = jnp.where(col >= core * overlap, val, 0.0)
+            inner[:, j * COL:(j + 1) * COL] = val.astype(BF)
+
+        for j in range(ff_chunks):
+            if j % GATE_WAIT == 0:
+                for jj in range(j, min(j + GATE_WAIT, ff_chunks)):
+                    for sub in range(2):
+                        gu_copy(l, jj, sub).wait()
+            sp = j % PAIRS
             hv = h[...]
             gate = dot(hv, ring[2 * sp])
             upper = dot(hv, ring[2 * sp + 1])
-            gate_block(jnp.maximum(j - 1, 0))
+            if j > 0:
+                gate_block(j - 1)
             raw[0] = gate
             raw[1] = upper
-
-            @pl.when(j + PAIRS < ff_chunks)
-            def _():
+            if j + PAIRS < ff_chunks:
                 for sub in range(2):
                     gu_copy(l, j + PAIRS, sub).start()
-
-            @pl.when((j + PAIRS >= ff_chunks) & (l + 1 < layers))
-            def _():
-                start_qkv(l + 1, sp)
-            return carry
-        lax.fori_loop(0, ff_chunks, gu_body, 0)
+            else:
+                @pl.when(l + 1 < layers)
+                def _(sp=sp):
+                    for sub in range(2):
+                        qkv_copy(l + 1, sp, (wq, wk, wv)[sp // 2], sub).start()
         gate_block(ff_chunks - 1)
 
-        def down_body(n, carry):
-            iv = inner[...]
-            for sub in range(OUT_COL // COL):
-                wd_copy(l, 2 * n + sub).wait()
+        for n in range(dim // COL):
+            wd_copy(l, n).wait()
+        iv = inner[...]
+        for n in range(n_col):
             for sub in range(OUT_COL // COL):
                 put_partial(n, sub * (COL // hd), dot(iv, wd_buf[2 * n + sub]))
             px_copy(1, n).start()
-            return carry
-        lax.fori_loop(0, dim // OUT_COL, down_body, 0)
         add_norm(1, gain_row(gain_a, lax.rem(l + 1, layers)))
         return carry
     lax.fori_loop(0, layers, layer, 0)
@@ -523,23 +549,23 @@
         smem = pl.BlockSpec(memory_space=pltpu.SMEM)
         dma = pltpu.SemaphoreType.DMA
         o_block = (half, tokens, hd)
-        s_block = (tokens, 128)
+        s_block, t_block = (tokens, 128), (8, 128)
         n_out = dim // OUT_COL
         scratch = [
             pltpu.VMEM((rows, dim), BF), pltpu.VMEM((rows, dim), BF), pltpu.VMEM((rows, half * hd), BF), pltpu.VMEM((rows, ff_cols), BF),
-            pltpu.VMEM((CHIPS, CORES, 2, half // 2, CORES, tokens, hd), BF),
+            pltpu.VMEM((CHIPS, CORES, CORES, half, tokens, hd), BF),
             pltpu.VMEM((half, CORES, tokens, hd), BF), pltpu.VMEM((half, CORES, tokens, hd), BF),
-            pltpu.VMEM((n_pages, 2, heads, page_len, hd), BF),
-            pltpu.VMEM((STAGE, 2, page_len, heads, hd), BF),
-            pltpu.VMEM((2, heads * PITCH, hd), F32),
+            pltpu.VMEM((n_pages, 2, page_len * heads, hd), BF),
+            pltpu.VMEM((TURN, 2, heads * PITCH, hd), F32),
             pltpu.VMEM((4, CORES) + o_block, F32), pltpu.VMEM((4, CORES) + o_block, F32), pltpu.VMEM((4, CORES) + o_block, F32),
             pltpu.VMEM((4, CORES) + s_block, F32), pltpu.VMEM((4, CORES) + s_block, F32), pltpu.VMEM((4, CORES) + s_block, F32),
+            pltpu.VMEM((4, CORES) + t_block, F32),
             pltpu.VMEM((CORES,) + o_block, F32), pltpu.VMEM((CORES,) + s_block, F32),
-            pltpu.VMEM((2,) + o_block, F32), pltpu.VMEM((2,) + s_block, F32),
-            pltpu.VMEM((2, CORES) + o_block, F32), pltpu.VMEM((2, CORES) + s_block, F32),
+            pltpu.VMEM((2,) + o_block, F32), pltpu.VMEM((2,) + t_block, F32),
+            pltpu.VMEM((2, CORES) + o_block, F32), pltpu.VMEM((2, CORES) + t_block, F32),
             pltpu.VMEM((2, n_out, CORES, OUT_COL // hd, tokens, hd), F32), pltpu.VMEM((2, rows, COL), F32),
             pltpu.VMEM((2 * PAIRS, dim, COL), BF), pltpu.VMEM((n_out, half * hd, OUT_COL), BF), pltpu.VMEM((dim // COL, ff_cols, COL), BF),
-            dma((2 * PAIRS,)), dma((n_out,)), dma((dim // COL,)), dma((STAGE,)),
+            dma((2 * PAIRS,)), dma((n_out,)), dma((dim // COL,)), dma((n_pages,)),
             dma((2,)), dma((8, 2)), dma((3, 2)), dma((3, 2)), dma((4, CORES, 2, 2)), dma((3, 3, 2)), dma((3, 3, 2)), dma((2, n_out, 2)),
         ]
         result = pl.pallas_call(
@@ -551,7 +577,7 @@
             compiler_params=pltpu.CompilerParams(collective_id=0, has_side_effects=True, vmem_limit_bytes=67043328),
             name="decoder",
         )(idx, hid, cos2, sin2, attn_norm, mlp_norm,
-          kv, w_query, w_key, w_value, w_out, w_gate, w_up, w_down)
+          kv.reshape(layers, n_pages, 2, page_len * heads, hd), w_query, w_key, w_value, w_out, w_gate, w_up, w_down)
         return result
 
     data_specs = (P(None, ("rep", "pool")), P(None, ("rep", "pool"), None), P(("rep", "pool")))

time: 163 us -> 143 us (0.88)
  Pallas kernels: 161 us -> 141 us
    pallas_call x1, Pallas kernels: 161 us -> 141 us  [local_program(): pl.pallas_call(functools.partial(kernel, cfg), out_shape=jax.ShapeDtypeSt...]
where the time goes in v3:
time: 143 us
  Pallas kernels  141 us (99%)
  local copies, waits for them, and re-layouts  1.67 us (1%)
    pallas_call x1, Pallas kernels, local_program(): pl.pallas_call(functools.partial(kernel, cfg), out_shape=jax.ShapeDtypeSt...  141 us

profile of v3, /device:TPU:113, one launch (start us, length us, event | category | flops | bytes accessed | tf_op | source)
XLA Modules:
  0.0 143.1 jit_solution(2844239332412284370)
XLA Ops:
  0.0 141.4 %decoder.1 = bf16[1,64,2048]{2,1,0:T(8,128)(2,1)} custom-call(s32[8,1,8]{2,1,0:T(1,128)} %idx.1, bf16[1,64,2048]{2,1,0:T(8,128)(2,1)} %hid.1, f32[128,128]{1,0:T(8,128)} %constant.4.clone.cos, f32[128,128]{1,0:T(8,128)} %constant.5.clone.sin, bf16[3,2048]{1,0:T(4,128)(2,1)} %gain_a.1, bf16[3,2048]{1,0:T(4,128)(2,1)} %gain_m.1, ...), custom_call_target="tpu_custom_call" | custom-call | tf_op jit(solution)/shard_map/decoder/pallas_call | solution.py:571
  141.4 1.7 %copy.16 = bf16[1,64,2048]{2,1,0:T(8,128)(2,1)} copy(bf16[1,64,2048]{2,1,0:T(8,128)(2,1)} %decoder.1) | data formatting | bytes 524288

commit v4 on v3

--- a/solution.py
+++ b/solution.py
@@ -407,16 +407,11 @@
         send(LEFT, 0, o_left(0))
         merge_pair(RIGHT, 1)
         send(RIGHT, 1, o_right(0))
-        q_part(3).wait_recv()
-        q_part(4).wait_recv()
         for n in range(n_col):
             wo_copy(l, n).start()
         for t in range(PAIRS):
             for sub in range(2):
                 gu_copy(l, t, sub).start()
-        attend_pages(near_last, other, p_send, s_send)
-        start(o_part(LEFT, 1))
-        start(o_part(RIGHT, 0))
         q_right(2).wait_recv()
         q_part(6).start()
         q_left(2).wait_recv()
@@ -427,15 +422,20 @@
         attend_pages(far_unit, other, p_send, s_send)
         start(o_part(FAR, 0))
         start(o_part(FAR, 1))
+        q_part(3).wait_recv()
+        q_part(4).wait_recv()
+        attend_pages(near_last, other, p_send, s_send)
+        start(o_part(LEFT, 1))
+        start(o_part(RIGHT, 0))
+        merge_pair(FAR, 0)
+        send(FAR, 0, o_right(1))
+        merge_pair(FAR, 1)
+        send(FAR, 1, o_left(1))
         q_part(0).wait_recv()
         q_part(1).wait_recv()
         attend_pages(own_unit, other, p_send, s_send)
         start(o_part(OWN, 0))
         start(o_part(OWN, 1))
-        merge_pair(FAR, 0)
-        send(FAR, 0, o_right(1))
-        merge_pair(FAR, 1)
-        send(FAR, 1, o_left(1))
 
         @pl.when(l + 1 < layers)
         def _():

time: 143 us -> 142 us (level)
  no operation moved by 1% of the time
where the time goes in v4:
time: 142 us
  Pallas kernels  140 us (99%)
  local copies, waits for them, and re-layouts  1.67 us (1%)
    pallas_call x1, Pallas kernels, local_program(): pl.pallas_call(functools.partial(kernel, cfg), out_shape=jax.ShapeDtypeSt...  140 us

profile of v4, /device:TPU:113, one launch (start us, length us, event | category | flops | bytes accessed | tf_op | source)
XLA Modules:
  0.0 141.9 jit_solution(3352324966918364977)
XLA Ops:
  0.0 140.2 %decoder.1 = bf16[1,64,2048]{2,1,0:T(8,128)(2,1)} custom-call(s32[8,1,8]{2,1,0:T(1,128)} %idx.1, bf16[1,64,2048]{2,1,0:T(8,128)(2,1)} %hid.1, f32[128,128]{1,0:T(8,128)} %constant.4.clone.cos, f32[128,128]{1,0:T(8,128)} %constant.5.clone.sin, bf16[3,2048]{1,0:T(4,128)(2,1)} %gain_a.1, bf16[3,2048]{1,0:T(4,128)(2,1)} %gain_m.1, ...), custom_call_target="tpu_custom_call" | custom-call | tf_op jit(solution)/shard_map/decoder/pallas_call | solution.py:571
  140.2 1.7 %copy.16 = bf16[1,64,2048]{2,1,0:T(8,128)(2,1)} copy(bf16[1,64,2048]{2,1,0:T(8,128)(2,1)} %decoder.1) | data formatting | bytes 524288
